TPU v7x, 256 devices: a whole 4x4x8 slice. The times are simulated.
256 devices in a mesh: dev: 128 (over x, z, y), rep: 2 (over core).
Axes of the slice: x: 4, y: 4, z: 8, core: 2. Of those that a mesh axis runs over, the one named last changes fastest.
Arguments:
- node_features: bfloat16 [8192, 2, 3136], P('dev', 'rep'), may hold values from -6 to 6
- src_node: int32 [128, 128, 2], P('dev'), may hold values from 0 to 63
- dst_node: int32 [128, 128, 2], P('dev'), may hold values from 0 to 63
- counts: int32 [128, 128], P('dev'), may hold values from 1 to 2, as said below
- rotation: bfloat16 [128, 128, 2, 235], P('dev'), may hold values from -2 to 2
- w_zero: bfloat16 [896, 2, 448], P(None, 'rep'), may hold values from -0.1875 to 0.1875
- w_one: bfloat16 [2, 768, 2, 384], P(None, None, 'rep'), may hold values from -0.15625 to 0.15625
- w_two: bfloat16 [2, 640, 2, 320], P(None, None, 'rep'), may hold values from -0.15625 to 0.15625
- norm_gain: float32 [2, 3136], P('rep'), may hold values from 0.5 to 1.5
Outputs:
- updated: bfloat16 [8192, 2, 3136], P('dev', 'rep')
Inputs may be any that keep to these rules, and one draw needn't show every extreme that they name: Slots i < counts[s, d] hold edges, the others padding; in every draw some destination device receives 2 edges from every source device.
All inputs are finite; a program needn't handle non-finite values.
Results may differ from a plain program's by a relative error of at most 0.0054.
Values may be sent and summed in bfloat16 or wider, within the bound.
A program may use at most 64 MiB of HBM per device.

v0:
```python
import math

import jax
import jax.numpy as jnp
from jax import lax
from jax.sharding import PartitionSpec as P


def for_sending(value):
    return jax.tree.map(lambda a: a.astype(jnp.bfloat16) if a.dtype == jnp.float32 else a, value)


def copy_for_each(value, axis):
    peers = lax.axis_size(axis)
    return lax.all_to_all(
        jnp.broadcast_to(value[None], (peers, *value.shape)), axis, 0, 0, tiled=True
    )


def laid_out(tiles, dim):
    shape = list(tiles.shape[1:])
    shape[dim] *= tiles.shape[0]
    return jnp.moveaxis(tiles, 0, dim).reshape(shape)


def gather_directly(value, axis, dim):
    tiles = copy_for_each(value, axis)
    return laid_out(tiles, dim)


def frame_slot(degree, order):
    if order == 0:
        return degree
    if order == 1:
        return 6 + degree
    if order == -1:
        return 12 + degree
    if order == 2:
        return 17 + degree
    return 22 + degree


def frame_tables():
    offsets = []
    places = []
    spot = 0
    for degree in range(7):
        reach = min(degree, 2)
        offsets.append(spot)
        spot += (2 * degree + 1) * (2 * reach + 1)
        places.append([frame_slot(degree, order) for order in range(-reach, reach + 1)])
    return (offsets, places)


def block_of(rotation, offsets, degree):
    reach = min(degree, 2)
    span = 2 * degree + 1
    height = 2 * reach + 1
    piece = rotation[:, offsets[degree] : offsets[degree] + height * span]
    return piece.reshape(rotation.shape[0], height, span).astype(jnp.float32)


def frame(coeffs, rotation):
    offsets, places = frame_tables()
    pieces = []
    for degree in range(7):
        matrix = block_of(rotation, offsets, degree)
        part = coeffs[:, degree * degree : degree * degree + 2 * degree + 1, :].astype(jnp.float32)
        pieces.append(jnp.sum(matrix[:, :, :, None] * part[:, None, :, :], axis=2))
    listing = sorted(
        (
            (places[degree][row], degree, row)
            for degree in range(7)
            for row in range(len(places[degree]))
        )
    )
    return jnp.concatenate(
        [pieces[degree][:, row : row + 1, :] for place, degree, row in listing], axis=1
    )


def unframe(framed, rotation):
    offsets, places = frame_tables()
    parts = []
    for degree in range(7):
        matrix = block_of(rotation, offsets, degree)
        chosen = jnp.concatenate(
            [framed[:, place : place + 1, :] for place in places[degree]], axis=1
        ).astype(jnp.float32)
        parts.append(jnp.sum(matrix[:, :, :, None] * chosen[:, :, None, :], axis=1))
    return jnp.concatenate(parts, axis=1)


def mix_orders(rotated, zero_mat, one_mats, two_mats):
    batch = rotated.shape[0]
    out_width = zero_mat.shape[1] // 7
    flat_zero = rotated[:, 0:7, :].reshape(batch, -1)
    result = [
        jnp.dot(flat_zero, zero_mat, preferred_element_type=jnp.float32).reshape(
            batch, 7, out_width
        )
    ]
    for first, count, mats in ((7, 6, one_mats), (19, 5, two_mats)):
        plus = rotated[:, first : first + count, :].reshape(batch, -1)
        minus = rotated[:, first + count : first + 2 * count, :].reshape(batch, -1)
        upper = jnp.dot(plus, mats[0], preferred_element_type=jnp.float32) - jnp.dot(
            minus, mats[1], preferred_element_type=jnp.float32
        )
        lower = jnp.dot(plus, mats[1], preferred_element_type=jnp.float32) + jnp.dot(
            minus, mats[0], preferred_element_type=jnp.float32
        )
        result.append(upper.reshape(batch, count, out_width))
        result.append(lower.reshape(batch, count, out_width))
    return jnp.concatenate(result, axis=1).astype(jnp.bfloat16)


def by_blocks(func, arrays, size):
    count = arrays[0].shape[0] // size
    shaped = tuple((member.reshape((count, size) + member.shape[1:]) for member in arrays))
    result = lax.map(lambda items: func(*items), shaped)
    return result.reshape((count * size,) + result.shape[2:])


def shards(node_features, src_node, dst_node, counts, rotation, w_zero, w_one, w_two, norm_gain):
    nodes = node_features.shape[0]
    flat = node_features.shape[2]
    half_width = flat // 49
    peers = src_node.shape[1]
    slots = src_node.shape[2]
    edges = peers * slots
    sources = src_node.reshape(edges)
    rot_rows = rotation.reshape(edges, 235)
    size = math.gcd(edges, 512)
    own = node_features.reshape(nodes, 49, half_width)

    def turn_half(index, rows):
        return frame(jnp.take(own, index, axis=0), rows).astype(jnp.bfloat16)

    own_rotated = by_blocks(turn_half, (sources, rot_rows), size)
    rotated = gather_directly(for_sending(own_rotated), "rep", 2).astype(own_rotated.dtype)
    zero_mat = w_zero.reshape(w_zero.shape[0], -1)
    one_mats = w_one.reshape(2, w_one.shape[1], -1)
    two_mats = w_two.reshape(2, w_two.shape[1], -1)
    live = (
        (jnp.arange(slots)[None, :] < counts.reshape(peers)[:, None])
        .reshape(edges)
        .astype(jnp.bfloat16)
    )

    def finish(block_rows, rows, alive):
        edge_out = mix_orders(block_rows, zero_mat, one_mats, two_mats)
        back = unframe(edge_out, rows).astype(jnp.bfloat16)
        return back * alive[:, None, None]

    outgoing = by_blocks(finish, (rotated, rot_rows, live), size).reshape(
        peers, slots, 49 * half_width
    )
    received = (
        lax.all_to_all(for_sending(outgoing), "dev", split_axis=0, concat_axis=0, tiled=True)
        .astype(outgoing.dtype)
        .reshape(edges, 49 * half_width)
    )
    targets = dst_node.reshape(edges)
    one_hot = (jnp.arange(nodes)[:, None] == targets[None, :]).astype(jnp.bfloat16)
    total = jnp.dot(one_hot, received, preferred_element_type=jnp.float32)
    partial_sq = jnp.sum(total * total, axis=1)
    summed_sq = lax.psum(partial_sq, "rep")
    mean_sq = summed_sq / (49 * half_width * lax.axis_size("rep"))
    normed = total * lax.rsqrt(mean_sq + 1e-06)[:, None]
    updated = node_features.reshape(nodes, flat).astype(jnp.float32) + norm_gain * normed
    return updated.astype(jnp.bfloat16).reshape(nodes, 1, flat)


def solution(mesh):
    return jax.shard_map(
        shards,
        mesh=mesh,
        in_specs=(
            P("dev", "rep", None),
            P("dev", None, None),
            P("dev", None, None),
            P("dev", None),
            P("dev", None, None, None),
            P(None, "rep", None),
            P(None, None, "rep", None),
            P(None, None, "rep", None),
            P("rep", None),
        ),
        out_specs=P("dev", "rep", None),
        check_vma=False,
    )
```

profile of v0, /device:TPU:1, one launch (start us, length us, event | category | flops | bytes accessed | tf_op | source)
XLA Modules:
  0.0 150.1 jit_solution(6904806285685543634)
XLA Ops:
  0.0 0.9 copy.111
  1.1 1.0 copy.110
  2.6 1.6 %reshape.639 = bf16[64,49,64]{2,1,0:T(8,128)(2,1)S(1)} reshape(bf16[64,1,3136]{2,0,1:T(8,128)(2,1)} %param.9) | data formatting | bytes 802816 | tf_op jit(solution)/shard_map/reshape | solution.py:134
  4.2 2.9 %gather_fusion = bf16[256,49,64]{2,1,0:T(8,128)(2,1)} fusion(bf16[64,49,64]{2,1,0:T(8,128)(2,1)S(1)} %reshape.639, s32[1024]{0:T(1024)S(1)} %pad_clamp_fusion), kind=kCustom, calls=%fused_computation | custom fusion | bytes 3212288 | tf_op jit(solution)/shard_map/while/body/eval_jaxpr/jit(_take)/gather | solution.py:137
  7.1 5.6 %copy.113 = bf16[256,49,64]{0,2,1:T(8,128)(2,1)} copy(bf16[256,49,64]{2,1,0:T(8,128)(2,1)} %gather_fusion) | data formatting | bytes 3211264 | tf_op jit(solution)/shard_map/while/body/eval_jaxpr/jit(_take)/gather | solution.py:137
  12.7 1.6 %broadcast_select_fusion = bf16[256,49,64]{0,2,1:T(8,128)(2,1)S(1)} fusion(bf16[256,49,64]{0,2,1:T(8,128)(2,1)} %copy.113, pred[256]{0:T(512)(128)(4,1)S(1)} %compare_and_fusion), kind=kLoop, calls=%fused_computation.11 | loop fusion | flops 802816 | bytes 3211520 | tf_op jit(solution)/shard_map/while/body/eval_jaxpr/jit(_take)/select_n | solution.py:137
  17.3 0.9 slice_convert_fusion.2
  18.9 0.9 slice_convert_fusion.1
  22.7 1.0 copy.129
  23.8 1.0 copy.130
  24.8 0.9 copy.131
  25.8 0.9 copy.132
  26.7 1.0 multiply_reduce_fusion.12
  28.3 1.1 multiply_reduce_fusion.9
  30.0 1.2 multiply_reduce_fusion.7
  47.7 1.5 broadcast_in_dim.89
  49.2 8.1 %all_to_all.10 = bf16[2,256,29,64]{1,3,2,0:T(8,128)(2,1)S(1)} all-to-all(bf16[2,256,29,64]{1,3,2,0:T(8,128)(2,1)S(1)} %broadcast_in_dim.89), channel_id=1, replica_groups=mesh['dev'=128,'rep'=2] {'rep'}, dimensions={0} | all-to-all | bytes 3801088 | tf_op jit(solution)/shard_map/all_to_all | solution.py:15
  57.7 1.1 copy-done.12
  59.2 1.1 fusion.9
  61.8 1.1 fusion.1
  62.8 1.1 copy.123
  63.9 2.2 %fusion = bf16[256,384]{1,0:T(8,128)(2,1)} fusion(f32[256,384]{1,0:T(8,128)} %fusion.9, bf16[256,768]{0,1:T(8,128)(2,1)S(1)} %bitcast.85, bf16[2,768,1,384]{3,1,2,0:T(8,128)(2,1)} %param.15), kind=kOutput, calls=%fused_computation.17 | convolution fusion | flops 151191552 | bytes 1572864 | tf_op jit(solution)/shard_map/while/body/eval_jaxpr/dot_general | solution.py:109
  66.1 1.1 copy.122
  70.6 6.7 %copy.124 = bf16[256,49,64]{2,1,0:T(8,128)(2,1)} copy(bf16[256,49,64]{0,2,1:T(8,128)(2,1)S(1)} %convert_dynamic-update-slice_fusion) | data formatting | bytes 3211264 | tf_op jit(solution)/shard_map/while/body/eval_jaxpr/concatenate | solution.py:91
  77.3 5.7 %convert_element_type.231 = bf16[128,2,3136]{2,1,0:T(2,128)(2,1)S(1)} reshape(bf16[256,49,64]{2,1,0:T(8,128)(2,1)} %copy.124) | data formatting | bytes 3211264 | tf_op jit(solution)/shard_map/while/body/eval_jaxpr/convert_element_type | solution.py:152
  83.2 2.7 %broadcast_multiply_fusion = bf16[128,2,3136]{2,1,0:T(2,128)(2,1)} fusion(bf16[128,2,3136]{2,1,0:T(2,128)(2,1)S(1)} %convert_element_type.231, bf16[128,2]{1,0:T(8,128)(2,1)S(1)} %fusion.27), kind=kLoop, calls=%fused_computation.24 | loop fusion | flops 802816 | bytes 3211776 | tf_op jit(solution)/shard_map/while/body/eval_jaxpr/mul | solution.py:153
  85.9 13.9 %all-to-all-start.1 = ((bf16[128,2,3136]{2,1,0:T(2,128)(2,1)}), bf16[128,2,3136]{2,1,0:T(2,128)(2,1)S(1)}, u32[]{:S(2)}, u32[]{:S(2)}) async-start(bf16[128,2,3136]{2,1,0:T(2,128)(2,1)} %broadcast_multiply_fusion), calls=%async_computation.1 | async-start | bytes 3276800 | tf_op jit(solution)/shard_map/all_to_all | solution.py:159
  100.1 39.4 %all-to-all-done.1 = bf16[128,2,3136]{2,1,0:T(2,128)(2,1)S(1)} async-done(((bf16[128,2,3136]{2,1,0:T(2,128)(2,1)}), bf16[128,2,3136]{2,1,0:T(2,128)(2,1)S(1)}, u32[]{:S(2)}, u32[]{:S(2)}) %all-to-all-start.1) | async-done | bytes 1605664 | tf_op jit(solution)/shard_map/all_to_all | solution.py:159
  139.6 2.2 %reshape.650 = bf16[256,3136]{1,0:T(8,128)(2,1)} reshape(bf16[128,2,3136]{2,1,0:T(2,128)(2,1)S(1)} %all-to-all-done.1) | data formatting | bytes 3211264 | tf_op jit(solution)/shard_map/reshape | solution.py:161
  141.7 2.0 %multiply_reduce_fusion.10 = (f32[64]{0:T(128)S(1)}, f32[64,3136]{1,0:T(8,128)S(1)}) fusion(bf16[256,3136]{1,0:T(8,128)(2,1)} %reshape.650, s32[256]{0:T(256)S(1)} %eq.16), kind=kOutput, calls=%fused_computation.23 | convolution fusion | flops 103178176 | bytes 2409728 | tf_op jit(solution)/shard_map/dot_general | solution.py:165
  143.7 5.4 %psum.7 = f32[64]{0:T(128)S(1)} all-reduce(f32[64]{0:T(128)S(1)} %get-tuple-element.77), channel_id=1, replica_groups=mesh['dev'=128,'rep'=2] {'rep'}, use_global_device_ids=true, to_apply=%region_13.14 | all-reduce | flops 64 | bytes 512 | tf_op jit(solution)/shard_map/psum | solution.py:167
  149.2 0.9 fusion.15
  (120 shorter events, 30.8 us)
Async XLA Ops:
  0.0 67.8 %copy-start = (bf16[896,1,448]{0,2,1:T(8,128)(2,1)S(1)}, bf16[896,1,448]{0,2,1:T(8,128)(2,1)}, u32[]{:S(2)}) copy-start(bf16[896,1,448]{0,2,1:T(8,128)(2,1)} %param.14) | copy-start | bytes 2408452
  22.6 9.2 %copy-start.3 = (f32[256,9,64]{0,2,1:T(8,128)S(1)}, f32[256,9,64]{0,2,1:T(8,128)}, u32[]{:S(2)}) copy-start(f32[256,9,64]{0,2,1:T(8,128)} %slice_convert_fusion.2) | copy-start | bytes 1769476
  23.7 8.9 %copy-start.2 = (f32[256,11,64]{0,2,1:T(8,128)S(1)}, f32[256,11,64]{0,2,1:T(8,128)}, u32[]{:S(2)}) copy-start(f32[256,11,64]{0,2,1:T(8,128)} %slice_convert_fusion.1) | copy-start | bytes 2162692
  23.8 7.4 %copy-start.6 = (f32[256,5,7]{0,2,1:T(8,128)}, f32[256,5,7]{0,2,1:T(8,128)S(1)}, u32[]{:S(2)}) copy-start(f32[256,5,7]{0,2,1:T(8,128)S(1)} %reshape.656) | copy-start | bytes 107524
  57.5 1.3 copy-start.12
  57.7 2.7 %copy-start.1 = (bf16[2,640,1,320]{1,3,2,0:T(8,128)(2,1)S(1)}, bf16[2,640,1,320]{1,3,2,0:T(8,128)(2,1)}, u32[]{:S(2)}) copy-start(bf16[2,640,1,320]{1,3,2,0:T(8,128)(2,1)} %param.16) | copy-start | bytes 2457604
  67.2 1.0 copy-start.5
  68.6 0.7 copy-start.8
  68.7 0.8 copy-start.7
  77.3 5.7 %copy-start.11 = (s32[1,128]{1,0:T(1,128)S(1)}, s32[1,128]{1,0:T(1,128)}, u32[]{:S(2)}) copy-start(s32[1,128]{1,0:T(1,128)} %param.12) | copy-start | bytes 1540
  85.9 14.0 %copy-start.10 = (s32[1,128,2]{1,2,0:T(2,128)S(1)}, s32[1,128,2]{1,2,0:T(2,128)}, u32[]{:S(2)}) copy-start(s32[1,128,2]{1,2,0:T(2,128)} %param.11) | copy-start | bytes 3076
  85.9 14.2 %copy-start.9 = (f32[1,3136]{1,0:T(1,128)S(1)}, f32[1,3136]{1,0:T(1,128)}, u32[]{:S(2)}) copy-start(f32[1,3136]{1,0:T(1,128)} %param.17) | copy-start | bytes 37636
  85.9 53.7 %all-to-all-start.1 = ((bf16[128,2,3136]{2,1,0:T(2,128)(2,1)}), bf16[128,2,3136]{2,1,0:T(2,128)(2,1)S(1)}, u32[]{:S(2)}, u32[]{:S(2)}) async-start(bf16[128,2,3136]{2,1,0:T(2,128)(2,1)} %broadcast_multiply_fusion), calls=%async_computation.1 | async-start | bytes 3276800 | tf_op jit(solution)/shard_map/all_to_all | solution.py:159
  141.7 7.4 %copy-start.4 = (bf16[64,1,3136]{2,0,1:T(8,128)(2,1)S(1)}, bf16[64,1,3136]{2,0,1:T(8,128)(2,1)}, u32[]{:S(2)}) copy-start(bf16[64,1,3136]{2,0,1:T(8,128)(2,1)} %param.9) | copy-start | bytes 1204228
where the time goes:
time: 151 us; the launch traced here: 150 us
  local copies, waits for them, and re-layouts  58.8 us (39%)
  waiting for transfers between devices  39.4 us (26%)
  other arithmetic  15.4 us (10%)
  starting transfers between devices  13.9 us (9%)
  blocking collectives  13.6 us (9%)
  matrix products  8.41 us (6%)
    all_to_all x1, waiting for transfers between devices, shards(): lax.all_to_all(for_sending(outgoing), 'dev', split_axis=0, concat_axis=0,...  39.4 us
    unnamed x70, local copies, waits for them, and re-layouts  24.5 us
    all_to_all x1, starting transfers between devices, shards(): lax.all_to_all(for_sending(outgoing), 'dev', split_axis=0, concat_axis=0,...  13.9 us
    gather x2, local copies, waits for them, and re-layouts, turn_half(): return frame(jnp.take(own, index, axis=0), rows).astype(jnp.bfloat16)  8.52 us
    all_to_all x1, blocking collectives, copy_for_each(): lax.all_to_all(jnp.broadcast_to(value[None], (peers, *value.shape)), axis...  8.15 us
    concatenate x2, local copies, waits for them, and re-layouts, unframe(): return jnp.concatenate(parts, axis=1)  6.73 us
    convert_element_type x1, local copies, waits for them, and re-layouts, finish(): back = unframe(edge_out, rows).astype(jnp.bfloat16)  5.73 us
    psum x1, blocking collectives, shards(): summed_sq = lax.psum(partial_sq, 'rep')  5.42 us
  transfers between devices with their start and end apart: 1, of which 1 were waited for; matrix products, arithmetic and copies ran while one was open for 0% of the time, Pallas kernels for 0%

commit v1 on v0

v1 whole, which is shorter than its diff:
```python
import functools

import jax
import jax.numpy as jnp
from jax import lax
from jax.experimental import pallas as pl
from jax.experimental.pallas import tpu as pltpu
from jax.sharding import PartitionSpec as P

MESH = pl.DeviceIdType.MESH
F32 = jnp.float32
BF16 = jnp.bfloat16

SLOTS = 128
ROWS = 256
CHUNKS = 4
CROWS = ROWS // CHUNKS
CSLOTS = SLOTS // CHUNKS
SELF = 7
TILES = 15
DEGREES = range(7)


def reach(l):
    return min(l, 2)


def frame_slot(degree, order):
    if order == 0:
        return degree
    if order == 1:
        return 6 + degree
    if order == -1:
        return 12 + degree
    if order == 2:
        return 17 + degree
    return 22 + degree


def arranged(l, a):
    start = sum((2 * m + 1) * (2 * reach(m) + 1) for m in range(l))
    spot = start + (a + reach(l)) * (2 * l + 1)
    return (0, spot) if l <= 4 else (1, spot - 115)


def message_places():
    place = {}
    for r in range(6):
        place[r] = (r // 2, r % 2)
    for r in range(7, 19):
        place[r] = (3 + (r - 7) // 2, (r - 7) % 2)
    for r in range(19, 23):
        place[r] = (9 + (r - 19) // 2, (r - 19) % 2)
    for r in range(24, 28):
        place[r] = (11 + (r - 24) // 2, (r - 24) % 2)
    place[23] = (13, 0)
    place[28] = (13, 1)
    place[6] = (14, 0)
    return place


PLACE = message_places()


def tiles_of(l):
    return range((l * l) // 2, ((l + 1) * (l + 1) - 1) // 2 + 1)


def pattern(lane, l, a, t):
    _, spot = arranged(l, a)
    picks = []
    for k in (2 * t, 2 * t + 1):
        b = k - l * l
        picks.append(spot + b if 0 <= b <= 2 * l else 127)
    return jnp.where(lane < 64, picks[0], picks[1])


def pick(table, index):
    return jnp.take_along_axis(table, index, axis=1, mode="promise_in_bounds")


def nt(a, b):
    return lax.dot_general(a, b, (((1,), (1,)), ((), ())), preferred_element_type=F32)


def nn(a, b):
    return jnp.dot(a, b, preferred_element_type=F32)


def z_step(k):
    return [4, 3, 5, 2, 6, 1, 7, 0][k]


def kernel(
    x_hbm, rt_hbm, src_hbm, dst_hbm, cnt_hbm, wz_hbm, w1_hbm, w2_hbm,
    agg_ref, sq_ref,
    xv, rtv, srcv, dstv, cntv, wz, w1, w2,
    rts, dtab, xs, own, packed, peer, full, msend, mrecv, dsend, drecv, back, sqs, sqr,
    load_sem, ps_sem, pr_sem, ms_sem, mr_sem, ds_sem, dr_sem, q_sem,
):
    me = lax.axis_index("dev")
    rep = lax.axis_index("rep")
    px, pz, py = me // 32, (me // 4) % 8, me % 4
    barrier = pltpu.get_barrier_semaphore()

    def greet(i, carry):
        pl.semaphore_signal(
            barrier, inc=1, device_id={"dev": (me + i + 1) % SLOTS}, device_id_type=MESH
        )
        return carry

    lax.fori_loop(0, SLOTS - 1, greet, 0)
    pl.semaphore_signal(barrier, inc=1, device_id={"rep": 1 - rep}, device_id_type=MESH)

    loads = [
        pltpu.make_async_copy(s, d, load_sem.at[i])
        for i, (s, d) in enumerate(
            [
                (rt_hbm, rtv), (src_hbm, srcv), (dst_hbm, dstv), (cnt_hbm, cntv), (x_hbm, xv),
                (wz_hbm, wz), (w1_hbm, w1), (w2_hbm, w2),
            ]
        )
    ]
    for copy in loads:
        copy.start()
    for copy in loads[:5]:
        copy.wait()

    def spot_of(sign):
        q = lax.broadcasted_iota(jnp.int32, (ROWS, ROWS), 0)
        col = lax.broadcasted_iota(jnp.int32, (ROWS, ROWS), 1)
        slot, i = q // 2, q % 2
        k, r = slot % 8, slot // 8
        h = (k + 1) // 2
        oz = jnp.where(k % 2 == 1, 4 - h, 4 + h)
        ox = r // 4
        oy = (r + r // 4) % 4
        tx = (px + sign * ox + 4) % 4
        tz = (pz + sign * oz + 8) % 8
        ty = (py + sign * oy + 4) % 4
        target = i * SLOTS + (tx * 8 + tz) * 4 + ty
        return jnp.where(col == target, 1.0, 0.0).astype(BF16)

    perm = spot_of(1)
    rts[...] = jnp.zeros_like(rts)
    for i in range(2):
        rts[0:235, i * 128 : (i + 1) * 128] = rtv[:, i, :].astype(F32)
    rows = lax.broadcasted_iota(jnp.int32, (256, 256), 0)
    cols = lax.broadcasted_iota(jnp.int32, (256, 256), 1)
    wanted = jnp.where(rows < 115, rows, jnp.where(rows < 128, 255, jnp.where(rows < 248, rows - 13, 255)))
    sel = jnp.where(wanted == cols, 1.0, 0.0).astype(BF16)
    rcat = nn(sel, rts[...].astype(BF16)).astype(BF16)
    table = nt(perm, rcat)
    dtab[...] = table
    dsend[...] = table.astype(BF16).reshape(SLOTS, 2, 256)

    node = lax.broadcasted_iota(jnp.int32, (64, 128), 0)
    hot = jnp.concatenate(
        [
            jnp.where((srcv[i : i + 1, :] == node) & (cntv[0:1, :] > i), 1.0, 0.0).astype(BF16)
            for i in range(2)
        ],
        axis=1,
    )
    hot_q = nt(perm, hot).astype(BF16)
    for s in range(7):
        xs[:, s * 448 : (s + 1) * 448] = nn(hot_q, xv[:, s * 448 : (s + 1) * 448])
    xs[:, 3136:3200] = jnp.zeros((ROWS, 64), F32)

    lane = lax.broadcasted_iota(jnp.int32, (CROWS, 128), 1)
    low = lane < 64

    def turn(c, carry):
        at = pl.ds(pl.multiple_of(c * CROWS, CROWS), CROWS)
        halves = {}
        for l in DEGREES:
            for a in range(-reach(l), reach(l) + 1):
                piece, _ = arranged(l, a)
                tab = dtab[at, piece * 128 : (piece + 1) * 128]
                acc = None
                for t in tiles_of(l):
                    term = pick(tab, pattern(lane, l, a, t)) * xs[at, t * 128 : (t + 1) * 128]
                    acc = term if acc is None else acc + term
                acc = acc + pltpu.roll(acc, 64, 1)
                row = frame_slot(l, a)
                own[at, row * 128 : (row + 1) * 128] = acc.astype(BF16)
        for t in range(TILES):
            first = own[at, 2 * t * 128 : (2 * t + 1) * 128].astype(F32)
            if t < 14:
                second = own[at, (2 * t + 1) * 128 : (2 * t + 2) * 128].astype(F32)
                first = jnp.where(low, first, second)
            packed[at, t * 128 : (t + 1) * 128] = first.astype(BF16)
        return carry

    lax.fori_loop(0, CHUNKS, turn, 0)

    pl.semaphore_wait(barrier, SLOTS)

    def to_peer(c):
        at = pl.ds(pl.multiple_of(c * CROWS, CROWS), CROWS)
        return pltpu.make_async_remote_copy(
            src_ref=packed.at[at],
            dst_ref=peer.at[at],
            send_sem=ps_sem.at[c],
            recv_sem=pr_sem.at[c],
            device_id={"rep": 1 - rep},
            device_id_type=MESH,
        )

    for c in range(CHUNKS):
        to_peer(c).start()

    tz = [(pz + z_step(k)) % 8 for k in range(8)]

    def send_chunk(c, source, target, send_sem, recv_sem):
        def group(g, carry):
            r = c * (CSLOTS // 8) + g
            tx = (px + r // 4) % 4
            ty = (py + r + r // 4) % 4
            for k in range(8):
                slot = r * 8 + k
                copy = pltpu.make_async_remote_copy(
                    src_ref=source.at[slot],
                    dst_ref=target.at[slot],
                    send_sem=send_sem.at[c],
                    recv_sem=recv_sem.at[c],
                    device_id={"dev": (tx * 8 + tz[k]) * 4 + ty},
                    device_id_type=MESH,
                )
                if k == SELF:

                    @pl.when(r > 0)
                    def _():
                        copy.start()
                else:
                    copy.start()
            return carry

        lax.fori_loop(0, CSLOTS // 8, group, 0)

    def wait_chunk(c, buffer, sem):
        @pl.when(c == 0)
        def _():
            part = buffer.at[pl.ds(0, CSLOTS - 1)]
            pltpu.make_async_copy(part, part, sem.at[0]).wait()

        @pl.when(c > 0)
        def _():
            part = buffer.at[pl.ds(c * CSLOTS, CSLOTS)]
            pltpu.make_async_copy(part, part, sem.at[c]).wait()

    lax.fori_loop(0, CHUNKS, lambda c, n: (send_chunk(c, dsend, drecv, ds_sem, dr_sem), n)[1], 0)
    drecv[SELF] = dsend[SELF]

    for copy in loads[5:]:
        copy.wait()

    mine = (lane // 64) == rep

    def mix(c, carry):
        at = pl.ds(pl.multiple_of(c * CROWS, CROWS), CROWS)
        to_peer(c).wait_recv()
        for t in range(TILES):
            got = peer[at, t * 128 : (t + 1) * 128].astype(F32)
            turned = pltpu.roll(got, 64, 1)
            for half in range(2):
                row = 2 * t + half
                if row < 29:
                    theirs = jnp.where(low, got, turned) if half == 0 else jnp.where(low, turned, got)
                    ours = own[at, row * 128 : (row + 1) * 128].astype(F32)
                    full[:, row * 128 : (row + 1) * 128] = jnp.where(mine, ours, theirs).astype(BF16)
        zero = nt(full[:, 0:896], wz[...])
        p1, m1 = full[:, 896:1664], full[:, 1664:2432]
        p2, m2 = full[:, 2432:3072], full[:, 3072:3712]
        plus1 = nn(p1, w1[0]) - nn(m1, w1[1])
        minus1 = nn(p1, w1[1]) + nn(m1, w1[0])
        plus2 = nt(p2, w2[0]) - nt(m2, w2[1])
        minus2 = nt(p2, w2[1]) + nt(m2, w2[0])
        last = jnp.concatenate([plus2[:, 256:320], minus2[:, 256:320]], axis=1)
        tail = jnp.concatenate([zero[:, 384:448], jnp.zeros((CROWS, 64), F32)], axis=1)
        message = jnp.concatenate(
            [zero[:, 0:384], plus1, minus1, plus2[:, 0:256], minus2[:, 0:256], last, tail], axis=1
        ).astype(BF16)
        spot = pl.ds(pl.multiple_of(c * CSLOTS, CSLOTS), CSLOTS)
        msend[spot] = message.reshape(CSLOTS, 2, TILES * 128)
        send_chunk(c, msend, mrecv, ms_sem, mr_sem)
        return carry

    lax.fori_loop(0, CHUNKS, mix, 0)
    mrecv[SELF] = msend[SELF]

    perm_back = spot_of(-1)
    hot_d = jnp.concatenate(
        [jnp.where(dstv[i : i + 1, :] == node, 1.0, 0.0).astype(BF16) for i in range(2)], axis=1
    )
    hot_n = nt(hot_d, perm_back).astype(BF16)

    def unturn(c, carry):
        at = pl.ds(pl.multiple_of(c * CROWS, CROWS), CROWS)
        spot = pl.ds(pl.multiple_of(c * CSLOTS, CSLOTS), CSLOTS)
        wait_chunk(c, drecv, dr_sem)
        wait_chunk(c, mrecv, mr_sem)
        dtab[at, :] = drecv[spot].reshape(CROWS, 256).astype(F32)
        xs[at, 0 : TILES * 128] = mrecv[spot].reshape(CROWS, TILES * 128).astype(F32)
        sums = {}

        def flush(t):
            back[at, t * 128 : (t + 1) * 128] = sums.pop(t).astype(BF16)

        for l in DEGREES:
            spread = {}
            for a in range(-reach(l), reach(l) + 1):
                tile, half = PLACE[frame_slot(l, a)]
                got = xs[at, tile * 128 : (tile + 1) * 128]
                turned = pltpu.roll(got, 64, 1)
                spread[a] = jnp.where(low, got, turned) if half == 0 else jnp.where(low, turned, got)
            for t in tiles_of(l):
                for a in range(-reach(l), reach(l) + 1):
                    piece, _ = arranged(l, a)
                    tab = dtab[at, piece * 128 : (piece + 1) * 128]
                    term = pick(tab, pattern(lane, l, a, t)) * spread[a]
                    sums[t] = sums[t] + term if t in sums else term
                if not (l < 6 and t in tiles_of(l + 1)):
                    flush(t)
        return carry

    lax.fori_loop(0, CHUNKS, unturn, 0)

    square = jnp.zeros((64, 1), F32)
    for s in range(7):
        part = nn(hot_n, back[:, s * 448 : (s + 1) * 448])
        agg_ref[:, s * 448 : (s + 1) * 448] = part
        square = square + jnp.sum(part * part, axis=1, keepdims=True)
    sqs[...] = jnp.broadcast_to(square, (64, 128))
    swap = pltpu.make_async_remote_copy(
        src_ref=sqs,
        dst_ref=sqr,
        send_sem=q_sem.at[0],
        recv_sem=q_sem.at[1],
        device_id={"rep": 1 - rep},
        device_id_type=MESH,
    )
    swap.start()
    for c in range(CHUNKS):
        to_peer(c).wait_send()
        wait_chunk(c, dsend, ds_sem)
        wait_chunk(c, msend, ms_sem)
    swap.wait()
    sq_ref[...] = sqs[...] + sqr[...]


def shards(node_features, src_node, dst_node, counts, rotation, w_zero, w_one, w_two, norm_gain):
    x = node_features.reshape(64, 3136)
    rt = rotation.transpose(0, 3, 2, 1).reshape(235, 2, 128)
    src = src_node.transpose(0, 2, 1).reshape(2, 128)
    dst = dst_node.transpose(0, 2, 1).reshape(2, 128)
    wz = w_zero.transpose(1, 2, 0).reshape(448, 896)
    w1 = w_one.reshape(2, 768, 384)
    w2 = w_two.transpose(0, 2, 3, 1).reshape(2, 320, 640)
    hbm = pl.BlockSpec(memory_space=pltpu.MemorySpace.HBM)
    vmem = pl.BlockSpec(memory_space=pltpu.VMEM)
    dma = pltpu.SemaphoreType.DMA
    agg, total = pl.pallas_call(
        kernel,
        out_shape=(
            jax.ShapeDtypeStruct((64, 3136), F32),
            jax.ShapeDtypeStruct((64, 128), F32),
        ),
        in_specs=[hbm] * 8,
        out_specs=(vmem, vmem),
        scratch_shapes=[
            pltpu.VMEM((64, 3136), BF16),
            pltpu.VMEM((235, 2, 128), BF16),
            pltpu.VMEM((2, 128), jnp.int32),
            pltpu.VMEM((2, 128), jnp.int32),
            pltpu.VMEM((1, 128), jnp.int32),
            pltpu.VMEM((448, 896), BF16),
            pltpu.VMEM((2, 768, 384), BF16),
            pltpu.VMEM((2, 320, 640), BF16),
            pltpu.VMEM((256, 256), F32),
            pltpu.VMEM((ROWS, 256), F32),
            pltpu.VMEM((ROWS, 3200), F32),
            pltpu.VMEM((ROWS, 29 * 128), BF16),
            pltpu.VMEM((ROWS, TILES * 128), BF16),
            pltpu.VMEM((ROWS, TILES * 128), BF16),
            pltpu.VMEM((CROWS, 29 * 128), BF16),
            pltpu.VMEM((SLOTS, 2, TILES * 128), BF16),
            pltpu.VMEM((SLOTS, 2, TILES * 128), BF16),
            pltpu.VMEM((SLOTS, 2, 256), BF16),
            pltpu.VMEM((SLOTS, 2, 256), BF16),
            pltpu.VMEM((ROWS, 3200), BF16),
            pltpu.VMEM((64, 128), F32),
            pltpu.VMEM((64, 128), F32),
            dma((8,)),
            dma((CHUNKS,)),
            dma((CHUNKS,)),
            dma((CHUNKS,)),
            dma((CHUNKS,)),
            dma((CHUNKS,)),
            dma((CHUNKS,)),
            dma((2,)),
        ],
        compiler_params=pltpu.CompilerParams(
            collective_id=0, has_side_effects=True, vmem_limit_bytes=48 * 2**20
        ),
    )(x, rt, src, dst, counts, wz, w1, w2)
    scale = lax.rsqrt(total[:, 0:1] / 6272.0 + 1e-06)
    updated = x.astype(F32) + norm_gain * (agg * scale)
    return updated.astype(BF16).reshape(64, 1, 3136)


def solution(mesh):
    return jax.shard_map(
        shards,
        mesh=mesh,
        in_specs=(
            P("dev", "rep", None),
            P("dev", None, None),
            P("dev", None, None),
            P("dev", None),
            P("dev", None, None, None),
            P(None, "rep", None),
            P(None, None, "rep", None),
            P(None, None, "rep", None),
            P("rep", None),
        ),
        out_specs=P("dev", "rep", None),
        check_vma=False,
    )
```

time: 151 us -> 67.9 us (0.45)
  Pallas kernels: 0 us -> 58.2 us
  local copies, waits for them, and re-layouts: 58.8 us -> 7.46 us
  waiting for transfers between devices: 39.4 us -> 0 us
  starting transfers between devices: 13.9 us -> 0 us
  blocking collectives: 13.6 us -> 0 us
  other arithmetic: 15.4 us -> 1.82 us
  matrix products: 8.41 us -> 0 us
    pallas_call x0 -> x1, Pallas kernels: none -> 58.2 us  [shards(): pl.pallas_call(kernel, out_shape=(jax.ShapeDtypeStruct((64, 3136), F32),...]
    all_to_all x1 -> x0, waiting for transfers between devices: 39.4 us -> none  [shards(): lax.all_to_all(for_sending(outgoing), 'dev', split_axis=0, concat_axis=0,...]
    unnamed x70 -> x16, local copies, waits for them, and re-layouts: 24.5 us -> 7.46 us
    all_to_all x1 -> x0, starting transfers between devices: 13.9 us -> none  [shards(): lax.all_to_all(for_sending(outgoing), 'dev', split_axis=0, concat_axis=0,...]
    gather x2 -> x0, local copies, waits for them, and re-layouts: 8.52 us -> none  [turn_half(): return frame(jnp.take(own, index, axis=0), rows).astype(jnp.bfloat16)]
    dot_general x10 -> x0, matrix products: 8.41 us -> none  [the longest x2 2.54 us: mix_orders(): jnp.dot(minus, mats[0], preferred_element_type=jnp.float32)]
    all_to_all x1 -> x0, blocking collectives: 8.15 us -> none  [copy_for_each(): lax.all_to_all(jnp.broadcast_to(value[None], (peers, *value.shape)), axis...]
    concatenate x4 -> x0, local copies, waits for them, and re-layouts: 7.35 us -> none  [the longest x2 6.73 us: unframe(): return jnp.concatenate(parts, axis=1)]
  transfers between devices with their start and end apart: 1 -> 0, of which waited for: 1 -> 0; matrix products, arithmetic and copies ran while one was open for 0% -> 0% of each run, Pallas kernels for 0% -> 0%
where the time goes in v1:
time: 67.9 us; the launch traced here: 67.6 us
  Pallas kernels  58.2 us (86%)
  local copies, waits for them, and re-layouts  7.46 us (11%)
  other arithmetic  1.82 us (3%)
    pallas_call x1, Pallas kernels, shards(): pl.pallas_call(kernel, out_shape=(jax.ShapeDtypeStruct((64, 3136), F32),...  58.2 us
    unnamed x16, local copies, waits for them, and re-layouts  7.46 us

profile of v1, /device:TPU:1, one launch (start us, length us, event | category | flops | bytes accessed | tf_op | source)
XLA Modules:
  0.0 67.6 jit_solution(5110084867030973645)
XLA Ops:
  0.0 0.7 %reduce = f32[3136]{0:T(1024)S(1)} reduce(f32[1,3136]{1,0:T(1,128)} %param.17, f32[]{:T(128)} %constant.14), dimensions={0}, to_apply=%param.17.reduce_sub_computation | reduce | bytes 25092 | tf_op args[8]
  0.7 0.0 copy-start
  0.8 1.0 %copy-done = bf16[64,1,3136]{2,0,1:T(8,128)(2,1)S(1)} copy-done((bf16[64,1,3136]{2,0,1:T(8,128)(2,1)S(1)}, bf16[64,1,3136]{2,0,1:T(8,128)(2,1)}, u32[]{:S(2)}) %copy-start) | copy-done | bytes 401432
  1.8 0.0 copy-start.1
  1.8 1.3 %copy-done.1 = bf16[2,768,1,384]{3,1,2,0:T(8,128)(2,1)S(1)} copy-done((bf16[2,768,1,384]{3,1,2,0:T(8,128)(2,1)S(1)}, bf16[2,768,1,384]{3,1,2,0:T(8,128)(2,1)}, u32[]{:S(2)}) %copy-start.1) | copy-done | bytes 1179672
  3.0 0.0 copy-start.2
  3.0 1.1 %copy-done.2 = bf16[2,640,1,320]{1,3,2,0:T(8,128)(2,1)S(1)} copy-done((bf16[2,640,1,320]{1,3,2,0:T(8,128)(2,1)S(1)}, bf16[2,640,1,320]{1,3,2,0:T(8,128)(2,1)}, u32[]{:S(2)}) %copy-start.2) | copy-done | bytes 819224
  4.2 0.0 copy-start.3
  4.2 1.1 %copy-done.3 = bf16[896,1,448]{0,2,1:T(8,128)(2,1)S(1)} copy-done((bf16[896,1,448]{0,2,1:T(8,128)(2,1)S(1)}, bf16[896,1,448]{0,2,1:T(8,128)(2,1)}, u32[]{:S(2)}) %copy-start.3) | copy-done | bytes 802840
  5.3 0.0 copy-start.4
  5.3 0.9 %copy-done.4 = bf16[1,128,2,235]{1,2,3,0:T(2,128)(2,1)S(1)} copy-done((bf16[1,128,2,235]{1,2,3,0:T(2,128)(2,1)S(1)}, bf16[1,128,2,235]{1,2,3,0:T(2,128)(2,1)}, u32[]{:S(2)}) %copy-start.4) | copy-done | bytes 120344
  6.2 0.0 copy-start.5
  6.2 0.7 %copy-done.5 = s32[1,128,2]{1,2,0:T(2,128)S(1)} copy-done((s32[1,128,2]{1,2,0:T(2,128)S(1)}, s32[1,128,2]{1,2,0:T(2,128)}, u32[]{:S(2)}) %copy-start.5) | copy-done | bytes 1048
  6.9 0.0 copy-start.6
  6.9 0.7 %copy-done.6 = s32[1,128,2]{1,2,0:T(2,128)S(1)} copy-done((s32[1,128,2]{1,2,0:T(2,128)S(1)}, s32[1,128,2]{1,2,0:T(2,128)}, u32[]{:S(2)}) %copy-start.6) | copy-done | bytes 1048
  7.6 0.0 copy-start.7
  7.6 0.7 copy-done.7
  8.2 58.2 %shard_map.91 = (f32[64,3136]{1,0:T(8,128)S(1)}, f32[64,128]{1,0:T(8,128)S(1)}) custom-call(bf16[64,3136]{1,0:T(8,128)(2,1)S(1)} %bitcast.22, bf16[235,2,128]{2,1,0:T(2,128)(2,1)S(1)} %bitcast.26, s32[2,128]{1,0:T(2,128)S(1)} %bitcast.27, s32[2,128]{1,0:T(2,128)S(1)} %bitcast.28, s32[1,128]{1,0:T(1,128)S(1)} %copy-done.7, bf16[448,896]{1,0:T(8,128)(2,1)S(1)} %bitcast.25, ...), custom_call_target="tpu_custom_call" | custom-call | tf_op jit(solution)/shard_map/pallas_call | solution.py:363
  66.5 0.1 rsqrt_reduce_fusion
  66.6 1.0 %fusion = bf16[64,1,3136]{2,0,1:T(8,128)(2,1)} fusion(f32[64,3136]{1,0:T(8,128)S(1)} %get-tuple-element.7, f32[64]{0:T(128)S(1)} %rsqrt_reduce_fusion, f32[3136]{0:T(1024)S(1)} %reduce, bf16[64,1,3136]{2,0,1:T(8,128)(2,1)S(1)} %copy-done), kind=kLoop, calls=%fused_computation.1 | loop fusion | flops 1003520 | bytes 1618432 | tf_op jit(solution)/shard_map/reshape | solution.py:409
Async XLA Ops:
  0.7 1.0 %copy-start = (bf16[64,1,3136]{2,0,1:T(8,128)(2,1)S(1)}, bf16[64,1,3136]{2,0,1:T(8,128)(2,1)}, u32[]{:S(2)}) copy-start(bf16[64,1,3136]{2,0,1:T(8,128)(2,1)} %param.9) | copy-start | bytes 1204228
  1.8 1.3 %copy-start.1 = (bf16[2,768,1,384]{3,1,2,0:T(8,128)(2,1)S(1)}, bf16[2,768,1,384]{3,1,2,0:T(8,128)(2,1)}, u32[]{:S(2)}) copy-start(bf16[2,768,1,384]{3,1,2,0:T(8,128)(2,1)} %param.15) | copy-start | bytes 3538948
  3.0 1.1 %copy-start.2 = (bf16[2,640,1,320]{1,3,2,0:T(8,128)(2,1)S(1)}, bf16[2,640,1,320]{1,3,2,0:T(8,128)(2,1)}, u32[]{:S(2)}) copy-start(bf16[2,640,1,320]{1,3,2,0:T(8,128)(2,1)} %param.16) | copy-start | bytes 2457604
  4.2 1.1 %copy-start.3 = (bf16[896,1,448]{0,2,1:T(8,128)(2,1)S(1)}, bf16[896,1,448]{0,2,1:T(8,128)(2,1)}, u32[]{:S(2)}) copy-start(bf16[896,1,448]{0,2,1:T(8,128)(2,1)} %param.14) | copy-start | bytes 2408452
  5.3 0.9 %copy-start.4 = (bf16[1,128,2,235]{1,2,3,0:T(2,128)(2,1)S(1)}, bf16[1,128,2,235]{1,2,3,0:T(2,128)(2,1)}, u32[]{:S(2)}) copy-start(bf16[1,128,2,235]{1,2,3,0:T(2,128)(2,1)} %param.13) | copy-start | bytes 360964
  6.2 0.7 %copy-start.5 = (s32[1,128,2]{1,2,0:T(2,128)S(1)}, s32[1,128,2]{1,2,0:T(2,128)}, u32[]{:S(2)}) copy-start(s32[1,128,2]{1,2,0:T(2,128)} %param.10) | copy-start | bytes 3076
  6.9 0.7 %copy-start.6 = (s32[1,128,2]{1,2,0:T(2,128)S(1)}, s32[1,128,2]{1,2,0:T(2,128)}, u32[]{:S(2)}) copy-start(s32[1,128,2]{1,2,0:T(2,128)} %param.11) | copy-start | bytes 3076
  7.6 0.7 copy-start.7

commit v2 on v1

v2 whole, which is shorter than its diff:
```python
import functools

import jax
import jax.numpy as jnp
from jax import lax
from jax.experimental import pallas as pl
from jax.experimental.pallas import tpu as pltpu
from jax.sharding import PartitionSpec as P

MESH = pl.DeviceIdType.MESH
F32 = jnp.float32
BF16 = jnp.bfloat16

SLOTS = 128
ROWS = 256
CHUNKS = 2
CROWS = ROWS // CHUNKS
CSLOTS = SLOTS // CHUNKS
SELF = 7
TILES = 15
WIDTH = 3136
DEGREES = range(7)


def reach(l):
    return min(l, 2)


def orders(l):
    return range(-reach(l), reach(l) + 1)


def frame_slot(degree, order):
    if order == 0:
        return degree
    if order == 1:
        return 6 + degree
    if order == -1:
        return 12 + degree
    if order == 2:
        return 17 + degree
    return 22 + degree


def entry(l, a, b):
    start = sum((2 * m + 1) * (2 * reach(m) + 1) for m in range(l))
    return start + (a + reach(l)) * (2 * l + 1) + b + l


def message_places():
    place = {}
    for r in range(6):
        place[r] = (r // 2, r % 2)
    for r in range(7, 19):
        place[r] = (3 + (r - 7) // 2, (r - 7) % 2)
    for r in range(19, 23):
        place[r] = (9 + (r - 19) // 2, (r - 19) % 2)
    for r in range(24, 28):
        place[r] = (11 + (r - 24) // 2, (r - 24) % 2)
    place[23] = (13, 0)
    place[28] = (13, 1)
    place[6] = (14, 0)
    return place


PLACE = message_places()


def nt(a, b):
    return lax.dot_general(a, b, (((1,), (1,)), ((), ())), preferred_element_type=F32)


def nn(a, b):
    return jnp.dot(a, b, preferred_element_type=F32)


def z_step(k):
    return [4, 3, 5, 2, 6, 1, 7, 0][k]


def unit(n):
    rows = lax.broadcasted_iota(jnp.int32, (n, n), 0)
    cols = lax.broadcasted_iota(jnp.int32, (n, n), 1)
    return jnp.where(rows == cols, 1.0, 0.0).astype(BF16)


def kernel(
    x_hbm, rt_hbm, src_hbm, dst_hbm, cnt_hbm, wz_hbm, w1_hbm, w2_hbm, gain_hbm,
    out_ref,
    xv, rtv, srcv, dstv, cntv, wz, w1, w2, gain,
    rts, dtab, xs, rot, msend, mrecv, dsend, drecv, back, agg, sqs, sqr,
    load_sem, ps_sem, pr_sem, ms_sem, mr_sem, ds_sem, dr_sem, q_sem,
):
    me = lax.axis_index("dev")
    rep = lax.axis_index("rep")
    px, pz, py = me // 32, (me // 4) % 8, me % 4
    barrier = pltpu.get_barrier_semaphore()

    loads = [
        pltpu.make_async_copy(s, d, load_sem.at[i])
        for i, (s, d) in enumerate(
            [
                (rt_hbm, rtv), (src_hbm, srcv), (dst_hbm, dstv), (cnt_hbm, cntv), (x_hbm, xv),
                (wz_hbm, wz), (w1_hbm, w1), (w2_hbm, w2), (gain_hbm, gain),
            ]
        )
    ]
    for copy in loads:
        copy.start()

    def greet(g, carry):
        for k in range(8):
            pl.semaphore_signal(
                barrier, inc=1, device_id={"dev": (me + g * 8 + k + 1) % SLOTS}, device_id_type=MESH
            )
        return carry

    lax.fori_loop(0, 15, greet, 0)
    for k in range(121, SLOTS):
        pl.semaphore_signal(barrier, inc=1, device_id={"dev": (me + k) % SLOTS}, device_id_type=MESH)
    pl.semaphore_signal(barrier, inc=1, device_id={"rep": 1 - rep}, device_id_type=MESH)

    def spot_of(sign):
        q = lax.broadcasted_iota(jnp.int32, (ROWS, 128), 0)
        col = lax.broadcasted_iota(jnp.int32, (ROWS, 128), 1)
        slot, i = q >> 1, q & 1
        k, r = slot & 7, slot >> 3
        h = (k + 1) >> 1
        oz = jnp.where((k & 1) == 1, 4 - h, 4 + h)
        ox = r >> 2
        oy = r + ox
        tx = (px + sign * ox + 8) & 3
        tz = (pz + sign * oz + 16) & 7
        ty = (py + sign * oy + 32) & 3
        target = tx * 32 + tz * 4 + ty
        hit = jnp.where(col == target, 1, 0)
        return jnp.concatenate(
            [jnp.where(i == side, hit, 0).astype(F32).astype(BF16) for side in range(2)], axis=1
        )

    perm = spot_of(1)
    eye = unit(128)
    node = lax.broadcasted_iota(jnp.int32, (64, 128), 0)

    for copy in loads[:5]:
        copy.wait()
    hot = jnp.concatenate(
        [
            jnp.where((srcv[i : i + 1, :] == node) & (cntv[0:1, :] > i), 1.0, 0.0).astype(BF16)
            for i in range(2)
        ],
        axis=1,
    )
    hot_q = nt(hot, perm).astype(BF16)
    for t in range(25):
        wide = 128 if t < 24 else 64
        turned = nt(eye[0:wide, 0:wide], xv[:, t * 128 : t * 128 + wide]).astype(BF16)
        xs[t * 128 : t * 128 + wide, :] = nn(turned, hot_q)

    rts[...] = jnp.zeros_like(rts)
    for i in range(2):
        rts[0:235, i * 128 : (i + 1) * 128] = rtv[:, i, :].astype(F32)
    table = rts[...].astype(BF16)
    dtab[...] = nt(table, perm)
    dsend[...] = nt(perm, table).astype(BF16).reshape(SLOTS, 2, 256)

    def lanes(c):
        return slice(c * 128, (c + 1) * 128)

    def turn(c):
        at = lanes(c)
        for l in DEGREES:
            sums = {}
            for b in range(-l, l + 1):
                k = l * l + l + b
                part = xs[k * 64 : (k + 1) * 64, at]
                for a in orders(l):
                    e = entry(l, a, b)
                    term = dtab[e : e + 1, at] * part
                    sums[a] = sums[a] + term if a in sums else term
            for a in orders(l):
                rot[c, frame_slot(l, a), rep] = sums[a].astype(BF16)

    def to_peer(c):
        return pltpu.make_async_remote_copy(
            src_ref=rot.at[c, :, rep],
            dst_ref=rot.at[c, :, rep],
            send_sem=ps_sem.at[c],
            recv_sem=pr_sem.at[c],
            device_id={"rep": 1 - rep},
            device_id_type=MESH,
        )

    tz = [(pz + z_step(k)) % 8 for k in range(8)]

    def send_chunk(c, source, target, send_sem, recv_sem):
        def group(g, carry):
            r = c * (CSLOTS // 8) + g
            tx = (px + r // 4) % 4
            ty = (py + r + r // 4) % 4
            for k in range(8):
                slot = r * 8 + k
                copy = pltpu.make_async_remote_copy(
                    src_ref=source.at[slot],
                    dst_ref=target.at[slot],
                    send_sem=send_sem.at[c],
                    recv_sem=recv_sem.at[c],
                    device_id={"dev": (tx * 8 + tz[k]) * 4 + ty},
                    device_id_type=MESH,
                )
                if k == SELF and c == 0:

                    @pl.when(r > 0)
                    def _():
                        copy.start()
                else:
                    copy.start()
            return carry

        lax.fori_loop(0, CSLOTS // 8, group, 0)

    def wait_chunk(c, buffer, sem):
        part = buffer.at[pl.ds(c * CSLOTS, CSLOTS - 1 if c == 0 else CSLOTS)]
        pltpu.make_async_copy(part, part, sem.at[c]).wait()

    def mix(c):
        to_peer(c).wait_recv()

        def rows(first, count):
            part = rot[c, first : first + count].reshape(count * 128, 128)
            return nt(eye, part).astype(BF16)

        zero = nt(rows(0, 7), wz[...])
        one = jnp.concatenate([rows(7, 6), rows(13, 6)], axis=0)
        two = jnp.concatenate([rows(19, 5), rows(24, 5)], axis=0)
        first, second = nn(one, w1[0]), nn(one, w1[1])
        plus1 = first[0:128] - second[128:256]
        minus1 = second[0:128] + first[128:256]
        first, second = nt(two, w2[0]), nt(two, w2[1])
        plus2 = first[0:128] - second[128:256]
        minus2 = second[0:128] + first[128:256]
        last = jnp.concatenate([plus2[:, 256:320], minus2[:, 256:320]], axis=1)
        tail = jnp.concatenate([zero[:, 384:448], jnp.zeros((CROWS, 64), F32)], axis=1)
        pieces = [zero[:, 0:384], plus1, minus1, plus2[:, 0:256], minus2[:, 0:256], last, tail]
        spot = 0
        for piece in pieces:
            wide = piece.shape[1]
            msend[c * CSLOTS : (c + 1) * CSLOTS, :, spot : spot + wide] = piece.astype(BF16).reshape(
                CSLOTS, 2, wide
            )
            spot += wide

    def unturn(c):
        at = lanes(c)
        wait_chunk(c, drecv, dr_sem)
        if c == 0:
            drecv[SELF] = dsend[SELF]
        rows = drecv[c * CSLOTS : (c + 1) * CSLOTS].reshape(CROWS, 256)
        dtab[0:128, at] = nt(eye, rows[:, 0:128])
        dtab[128:256, at] = nt(eye, rows[:, 128:256])
        wait_chunk(c, mrecv, mr_sem)
        if c == 0:
            mrecv[SELF] = msend[SELF]
        for t in range(TILES):
            tile = mrecv[c * CSLOTS : (c + 1) * CSLOTS, :, t * 128 : (t + 1) * 128].reshape(CROWS, 128)
            xs[t * 128 : (t + 1) * 128, at] = nt(eye, tile)
        for l in DEGREES:
            parts = {}
            for a in orders(l):
                tile, half = PLACE[frame_slot(l, a)]
                spot = (2 * tile + half) * 64
                parts[a] = xs[spot : spot + 64, at]
            for b in range(-l, l + 1):
                total = None
                for a in orders(l):
                    e = entry(l, a, b)
                    term = dtab[e : e + 1, at] * parts[a]
                    total = term if total is None else total + term
                k = l * l + l + b
                back[k * 64 : (k + 1) * 64, at] = total.astype(BF16)

    for c in range(CHUNKS):
        turn(c)

    pl.semaphore_wait(barrier, SLOTS)
    for c in range(CHUNKS):
        to_peer(c).start()
    for c in range(CHUNKS):
        send_chunk(c, dsend, drecv, ds_sem, dr_sem)

    for copy in loads[5:]:
        copy.wait()
    for c in range(CHUNKS):
        mix(c)
        send_chunk(c, msend, mrecv, ms_sem, mr_sem)

    perm_back = spot_of(-1)
    hot_d = jnp.concatenate(
        [jnp.where(dstv[i : i + 1, :] == node, 1.0, 0.0).astype(BF16) for i in range(2)], axis=1
    )
    hot_n = nt(hot_d, perm_back).astype(BF16)

    for c in range(CHUNKS):
        unturn(c)

    square = jnp.zeros((64, 1), F32)
    for s in range(7):
        at = slice(s * 448, (s + 1) * 448)
        part = nt(hot_n, back[at, :])
        agg[:, at] = part
        square = square + jnp.sum(part * part, axis=1, keepdims=True)
    sqs[...] = jnp.broadcast_to(square, (64, 128))
    swap = pltpu.make_async_remote_copy(
        src_ref=sqs,
        dst_ref=sqr,
        send_sem=q_sem.at[0],
        recv_sem=q_sem.at[1],
        device_id={"rep": 1 - rep},
        device_id_type=MESH,
    )
    swap.start()
    for c in range(CHUNKS):
        to_peer(c).wait_send()
        wait_chunk(c, dsend, ds_sem)
        wait_chunk(c, msend, ms_sem)
    swap.wait()
    mean = (sqs[...] + sqr[...]) / 6272.0
    scale = lax.rsqrt(mean + 1e-06)[:, 0:1]
    for s in range(7):
        at = slice(s * 448, (s + 1) * 448)
        normed = agg[:, at] * scale
        out_ref[:, at] = (xv[:, at].astype(F32) + gain[0:1, at] * normed).astype(BF16)


def shards(node_features, src_node, dst_node, counts, rotation, w_zero, w_one, w_two, norm_gain):
    x = node_features.reshape(64, WIDTH)
    rt = rotation.transpose(0, 3, 2, 1).reshape(235, 2, 128)
    src = src_node.transpose(0, 2, 1).reshape(2, 128)
    dst = dst_node.transpose(0, 2, 1).reshape(2, 128)
    wz = w_zero.transpose(1, 2, 0).reshape(448, 896)
    w1 = w_one.reshape(2, 768, 384)
    w2 = w_two.transpose(0, 2, 3, 1).reshape(2, 320, 640)
    hbm = pl.BlockSpec(memory_space=pltpu.MemorySpace.HBM)
    vmem = pl.BlockSpec(memory_space=pltpu.VMEM)
    dma = pltpu.SemaphoreType.DMA
    updated = pl.pallas_call(
        kernel,
        out_shape=jax.ShapeDtypeStruct((64, WIDTH), BF16),
        in_specs=[hbm] * 9,
        out_specs=vmem,
        scratch_shapes=[
            pltpu.VMEM((64, WIDTH), BF16),
            pltpu.VMEM((235, 2, 128), BF16),
            pltpu.VMEM((2, 128), jnp.int32),
            pltpu.VMEM((2, 128), jnp.int32),
            pltpu.VMEM((1, 128), jnp.int32),
            pltpu.VMEM((448, 896), BF16),
            pltpu.VMEM((2, 768, 384), BF16),
            pltpu.VMEM((2, 320, 640), BF16),
            pltpu.VMEM((1, WIDTH), F32),
            pltpu.VMEM((256, 256), F32),
            pltpu.VMEM((256, ROWS), F32),
            pltpu.VMEM((WIDTH, ROWS), F32),
            pltpu.VMEM((CHUNKS, 29, 2, 64, 128), BF16),
            pltpu.VMEM((SLOTS, 2, TILES * 128), BF16),
            pltpu.VMEM((SLOTS, 2, TILES * 128), BF16),
            pltpu.VMEM((SLOTS, 2, 256), BF16),
            pltpu.VMEM((SLOTS, 2, 256), BF16),
            pltpu.VMEM((WIDTH, ROWS), BF16),
            pltpu.VMEM((64, WIDTH), F32),
            pltpu.VMEM((64, 128), F32),
            pltpu.VMEM((64, 128), F32),
            dma((9,)),
            dma((CHUNKS,)),
            dma((CHUNKS,)),
            dma((CHUNKS,)),
            dma((CHUNKS,)),
            dma((CHUNKS,)),
            dma((CHUNKS,)),
            dma((2,)),
        ],
        compiler_params=pltpu.CompilerParams(
            collective_id=0, has_side_effects=True, vmem_limit_bytes=67043328
        ),
    )(x, rt, src, dst, counts, wz, w1, w2, norm_gain)
    return updated.reshape(64, 1, WIDTH)


def solution(mesh):
    return jax.shard_map(
        shards,
        mesh=mesh,
        in_specs=(
            P("dev", "rep", None),
            P("dev", None, None),
            P("dev", None, None),
            P("dev", None),
            P("dev", None, None, None),
            P(None, "rep", None),
            P(None, None, "rep", None),
            P(None, None, "rep", None),
            P("rep", None),
        ),
        out_specs=P("dev", "rep", None),
        check_vma=False,
    )
```

time: 67.9 us -> 47.2 us (0.70)
  Pallas kernels: 58.2 us -> 45.3 us
  local copies, waits for them, and re-layouts: 7.46 us -> 1.78 us
  other arithmetic: 1.82 us -> 0 us
    pallas_call x1, Pallas kernels: 58.2 us -> 45.3 us  [shards(): pl.pallas_call(kernel, out_shape=jax.ShapeDtypeStruct((64, WIDTH), BF16),...]
    unnamed x16 -> x1, local copies, waits for them, and re-layouts: 7.46 us -> 1.78 us
    reshape x1 -> x0, other arithmetic: 0.96 us -> none  [shards(): return updated.astype(BF16).reshape(64, 1, 3136)]
    unnamed x1 -> x0, other arithmetic: 0.74 us -> none
where the time goes in v2:
time: 47.2 us; the launch traced here: 47.1 us
  Pallas kernels  45.3 us (96%)
  local copies, waits for them, and re-layouts  1.78 us (4%)
    pallas_call x1, Pallas kernels, shards(): pl.pallas_call(kernel, out_shape=jax.ShapeDtypeStruct((64, WIDTH), BF16),...  45.3 us
    unnamed x1, local copies, waits for them, and re-layouts  1.78 us

profile of v2, /device:TPU:1, one launch (start us, length us, event | category | flops | bytes accessed | tf_op | source)
XLA Modules:
  0.0 47.1 jit_solution(16109478829914808034)
XLA Ops:
  0.0 45.3 %shard_map.91 = bf16[64,3136]{1,0:T(8,128)(2,1)} custom-call(bf16[64,3136]{1,0:T(8,128)(2,1)} %bitcast.24, bf16[235,2,128]{2,1,0:T(2,128)(2,1)} %bitcast.25, s32[2,128]{1,0:T(2,128)} %bitcast.26, s32[2,128]{1,0:T(2,128)} %bitcast.27, s32[1,128]{1,0:T(1,128)} %cnt_hbm.1, bf16[448,896]{1,0:T(8,128)(2,1)} %bitcast.23, bf16[2,768,384]{2,1,0:T(8,128)(2,1)} %bitcast.21, ...), custom_call_target="tpu_custom_call" | custom-call | tf_op jit(solution)/shard_map/pallas_call | solution.py:346
  45.3 1.8 %copy.12 = bf16[64,1,3136]{2,0,1:T(8,128)(2,1)} copy(bf16[64,1,3136]{2,0,1:T(8,128)(2,1)} %bitcast.20) | data formatting | bytes 802816

commit v3 on v2

--- a/solution.py
+++ b/solution.py
@@ -16,9 +16,9 @@
 CHUNKS = 2
 CROWS = ROWS // CHUNKS
 CSLOTS = SLOTS // CHUNKS
-SELF = 7
 TILES = 15
 WIDTH = 3136
+LEAD = ((0, 1), (1, 3), (2, 4))
 DEGREES = range(7)
 
 
@@ -74,10 +74,6 @@
     return jnp.dot(a, b, preferred_element_type=F32)
 
 
-def z_step(k):
-    return [4, 3, 5, 2, 6, 1, 7, 0][k]
-
-
 def unit(n):
     rows = lax.broadcasted_iota(jnp.int32, (n, n), 0)
     cols = lax.broadcasted_iota(jnp.int32, (n, n), 1)
@@ -124,9 +120,7 @@
         q = lax.broadcasted_iota(jnp.int32, (ROWS, 128), 0)
         col = lax.broadcasted_iota(jnp.int32, (ROWS, 128), 1)
         slot, i = q >> 1, q & 1
-        k, r = slot & 7, slot >> 3
-        h = (k + 1) >> 1
-        oz = jnp.where((k & 1) == 1, 4 - h, 4 + h)
+        oz, r = slot & 7, slot >> 3
         ox = r >> 2
         oy = r + ox
         tx = (px + sign * ox + 8) & 3
@@ -191,33 +185,38 @@
             device_id_type=MESH,
         )
 
-    tz = [(pz + z_step(k)) % 8 for k in range(8)]
-
-    def send_chunk(c, source, target, send_sem, recv_sem):
-        def group(g, carry):
-            r = c * (CSLOTS // 8) + g
-            tx = (px + r // 4) % 4
-            ty = (py + r + r // 4) % 4
-            for k in range(8):
-                slot = r * 8 + k
-                copy = pltpu.make_async_remote_copy(
-                    src_ref=source.at[slot],
-                    dst_ref=target.at[slot],
-                    send_sem=send_sem.at[c],
-                    recv_sem=recv_sem.at[c],
-                    device_id={"dev": (tx * 8 + tz[k]) * 4 + ty},
-                    device_id_type=MESH,
-                )
-                if k == SELF and c == 0:
-
-                    @pl.when(r > 0)
-                    def _():
-                        copy.start()
-                else:
-                    copy.start()
+    def send(r, plane, allowed, source, target, send_sem, recv_sem):
+        tx = (px + (r >> 2)) & 3
+        ty = (py + r + (r >> 2)) & 3
+        slot = r * 8 + ((plane - pz) & 7)
+        copy = pltpu.make_async_remote_copy(
+            src_ref=source.at[slot],
+            dst_ref=target.at[slot],
+            send_sem=send_sem.at[r >> 3],
+            recv_sem=recv_sem.at[r >> 3],
+            device_id={"dev": tx * 32 + plane * 4 + ty},
+            device_id_type=MESH,
+        )
+
+        @pl.when(allowed & (slot > 0))
+        def _():
+            copy.start()
+
+    planes = [(pz + step) & 7 for step in (4, 3, 5, 2, 6, 1, 7, 0)]
+
+    def send_steps(first, last, buffers, lead):
+        def step(t, carry):
+            for plane in planes:
+                r = t
+                for early, gap in lead:
+                    r = r + jnp.where(plane == early, t // gap, 0)
+                send(r, plane, r < 16, *buffers)
+            for early, gap in lead:
+                r = t + t // gap + 1
+                send(r, early, (t % gap == gap - 1) & (r < 16), *buffers)
             return carry
 
-        lax.fori_loop(0, CSLOTS // 8, group, 0)
+        lax.fori_loop(first, last, step, 0)
 
     def wait_chunk(c, buffer, sem):
         part = buffer.at[pl.ds(c * CSLOTS, CSLOTS - 1 if c == 0 else CSLOTS)]
@@ -254,13 +253,13 @@
         at = lanes(c)
         wait_chunk(c, drecv, dr_sem)
         if c == 0:
-            drecv[SELF] = dsend[SELF]
+            drecv[0] = dsend[0]
         rows = drecv[c * CSLOTS : (c + 1) * CSLOTS].reshape(CROWS, 256)
         dtab[0:128, at] = nt(eye, rows[:, 0:128])
         dtab[128:256, at] = nt(eye, rows[:, 128:256])
         wait_chunk(c, mrecv, mr_sem)
         if c == 0:
-            mrecv[SELF] = msend[SELF]
+            mrecv[0] = msend[0]
         for t in range(TILES):
             tile = mrecv[c * CSLOTS : (c + 1) * CSLOTS, :, t * 128 : (t + 1) * 128].reshape(CROWS, 128)
             xs[t * 128 : (t + 1) * 128, at] = nt(eye, tile)
@@ -285,14 +284,14 @@
     pl.semaphore_wait(barrier, SLOTS)
     for c in range(CHUNKS):
         to_peer(c).start()
-    for c in range(CHUNKS):
-        send_chunk(c, dsend, drecv, ds_sem, dr_sem)
+    send_steps(0, 16, (dsend, drecv, ds_sem, dr_sem), ())
 
     for copy in loads[5:]:
         copy.wait()
-    for c in range(CHUNKS):
-        mix(c)
-        send_chunk(c, msend, mrecv, ms_sem, mr_sem)
+    mix(0)
+    send_steps(0, 4, (msend, mrecv, ms_sem, mr_sem), LEAD)
+    mix(1)
+    send_steps(4, 16, (msend, mrecv, ms_sem, mr_sem), LEAD)
 
     perm_back = spot_of(-1)
     hot_d = jnp.concatenate(
@@ -300,15 +299,17 @@
     )
     hot_n = nt(hot_d, perm_back).astype(BF16)
 
+    square = jnp.zeros((64, 1), F32)
     for c in range(CHUNKS):
         unturn(c)
-
-    square = jnp.zeros((64, 1), F32)
-    for s in range(7):
-        at = slice(s * 448, (s + 1) * 448)
-        part = nt(hot_n, back[at, :])
-        agg[:, at] = part
-        square = square + jnp.sum(part * part, axis=1, keepdims=True)
+        for s in range(7):
+            at = slice(s * 448, (s + 1) * 448)
+            part = nt(hot_n[:, lanes(c)], back[at, lanes(c)])
+            if c > 0:
+                part = agg[:, at] + part
+            agg[:, at] = part
+            if c == CHUNKS - 1:
+                square = square + jnp.sum(part * part, axis=1, keepdims=True)
     sqs[...] = jnp.broadcast_to(square, (64, 128))
     swap = pltpu.make_async_remote_copy(
         src_ref=sqs,
@@ -380,9 +381,9 @@
             dma((2,)),
         ],
         compiler_params=pltpu.CompilerParams(
-            collective_id=0, has_side_effects=True, vmem_limit_bytes=67043328
+            collective_id=0, has_side_effects=True, vmem_limit_bytes=40000000
         ),
-    )(x, rt, src, dst, counts, wz, w1, w2, norm_gain)
+    )(*[pltpu.with_memory_space_constraint(v, pltpu.MemorySpace.HBM) for v in (x, rt, src, dst, counts, wz, w1, w2, norm_gain)])
     return updated.reshape(64, 1, WIDTH)
 
 

time: 47.2 us -> 43.7 us (0.926)
  the two profiles are of different devices: /device:TPU:1 before, /device:TPU:35 now
where the time goes in v3:
time: 43.7 us; the launch traced here: 43.6 us
  Pallas kernels  42.8 us (98%)
  local copies, waits for them, and re-layouts  0.75 us (2%)
    pallas_call x1, Pallas kernels, shards(): pl.pallas_call(kernel, out_shape=jax.ShapeDtypeStruct((64, WIDTH), BF16),...  42.8 us

profile of v3, /device:TPU:35, one launch (start us, length us, event | category | flops | bytes accessed | tf_op | source)
XLA Modules:
  0.0 43.6 jit_solution(9623836166357705771)
XLA Ops:
  0.0 42.8 %shard_map.91 = bf16[64,3136]{1,0:T(8,128)(2,1)S(1)} custom-call(bf16[64,3136]{1,0:T(8,128)(2,1)} %bitcast.24, bf16[235,2,128]{2,1,0:T(2,128)(2,1)} %bitcast.25, s32[2,128]{1,0:T(2,128)} %bitcast.26, s32[2,128]{1,0:T(2,128)} %bitcast.27, s32[1,128]{1,0:T(1,128)} %cnt_hbm.1, bf16[448,896]{1,0:T(8,128)(2,1)} %bitcast.23, bf16[2,768,384]{2,1,0:T(8,128)(2,1)} %bitcast.21, ...), custom_call_target="tpu_custom_call" | custom-call | tf_op jit(solution)/shard_map/pallas_call | solution.py:347
  42.8 0.8 %copy.12 = bf16[64,1,3136]{2,0,1:T(8,128)(2,1)} copy(bf16[64,1,3136]{2,0,1:T(8,128)(2,1)S(1)} %bitcast.20) | data formatting | bytes 802816

commit v4 on v3

--- a/solution.py
+++ b/solution.py
@@ -16,9 +16,11 @@
 CHUNKS = 2
 CROWS = ROWS // CHUNKS
 CSLOTS = SLOTS // CHUNKS
-TILES = 15
+ZERO_TILES = 4
+REST_TILES = 11
+TILES = ZERO_TILES + REST_TILES
 WIDTH = 3136
-LEAD = ((0, 1), (1, 3), (2, 4))
+LEAD = ((0, 1), (1, 2), (2, 3), (3, 6))
 DEGREES = range(7)
 
 
@@ -49,17 +51,16 @@
 
 def message_places():
     place = {}
-    for r in range(6):
+    for r in range(7):
         place[r] = (r // 2, r % 2)
     for r in range(7, 19):
-        place[r] = (3 + (r - 7) // 2, (r - 7) % 2)
+        place[r] = (ZERO_TILES + (r - 7) // 2, (r - 7) % 2)
     for r in range(19, 23):
-        place[r] = (9 + (r - 19) // 2, (r - 19) % 2)
+        place[r] = (ZERO_TILES + 6 + (r - 19) // 2, (r - 19) % 2)
     for r in range(24, 28):
-        place[r] = (11 + (r - 24) // 2, (r - 24) % 2)
-    place[23] = (13, 0)
-    place[28] = (13, 1)
-    place[6] = (14, 0)
+        place[r] = (ZERO_TILES + 8 + (r - 24) // 2, (r - 24) % 2)
+    place[23] = (ZERO_TILES + 10, 0)
+    place[28] = (ZERO_TILES + 10, 1)
     return place
 
 
@@ -84,13 +85,30 @@
     x_hbm, rt_hbm, src_hbm, dst_hbm, cnt_hbm, wz_hbm, w1_hbm, w2_hbm, gain_hbm,
     out_ref,
     xv, rtv, srcv, dstv, cntv, wz, w1, w2, gain,
-    rts, dtab, xs, rot, msend, mrecv, dsend, drecv, back, agg, sqs, sqr,
-    load_sem, ps_sem, pr_sem, ms_sem, mr_sem, ds_sem, dr_sem, q_sem,
+    rts, dtab, xs, rot, zsend, zrecv, msend, mrecv, dsend, drecv, dswap, back, agg, sqs, sqr,
+    load_sem, ps_sem, pr_sem, zs_sem, zr_sem, ms_sem, mr_sem, ds_sem, dr_sem, ws_sem, wr_sem, q_sem,
 ):
     me = lax.axis_index("dev")
     rep = lax.axis_index("rep")
     px, pz, py = me // 32, (me // 4) % 8, me % 4
     barrier = pltpu.get_barrier_semaphore()
+
+    def greet(g, carry):
+        tx = (px + 2 + (g >> 2)) & 3
+        ty = (py + 2 + g) & 3
+        for step in (4, 3, 5, 2, 6, 1, 7):
+            spot = tx * 32 + ((pz + step) & 7) * 4 + ty
+            pl.semaphore_signal(barrier, inc=1, device_id={"dev": spot}, device_id_type=MESH)
+
+        @pl.when(g != 10)
+        def _():
+            spot = tx * 32 + pz * 4 + ty
+            pl.semaphore_signal(barrier, inc=1, device_id={"dev": spot}, device_id_type=MESH)
+
+        return carry
+
+    lax.fori_loop(0, 16, greet, 0)
+    pl.semaphore_signal(barrier, inc=1, device_id={"rep": 1 - rep}, device_id_type=MESH)
 
     loads = [
         pltpu.make_async_copy(s, d, load_sem.at[i])
@@ -103,18 +121,6 @@
     ]
     for copy in loads:
         copy.start()
-
-    def greet(g, carry):
-        for k in range(8):
-            pl.semaphore_signal(
-                barrier, inc=1, device_id={"dev": (me + g * 8 + k + 1) % SLOTS}, device_id_type=MESH
-            )
-        return carry
-
-    lax.fori_loop(0, 15, greet, 0)
-    for k in range(121, SLOTS):
-        pl.semaphore_signal(barrier, inc=1, device_id={"dev": (me + k) % SLOTS}, device_id_type=MESH)
-    pl.semaphore_signal(barrier, inc=1, device_id={"rep": 1 - rep}, device_id_type=MESH)
 
     def spot_of(sign):
         q = lax.broadcasted_iota(jnp.int32, (ROWS, 128), 0)
@@ -156,36 +162,56 @@
         rts[0:235, i * 128 : (i + 1) * 128] = rtv[:, i, :].astype(F32)
     table = rts[...].astype(BF16)
     dtab[...] = nt(table, perm)
-    dsend[...] = nt(perm, table).astype(BF16).reshape(SLOTS, 2, 256)
+    half = rts[pl.ds(pl.multiple_of(rep * 128, 128), 128), :].astype(BF16)
+    dsend[...] = nt(perm, half).astype(BF16).reshape(SLOTS, 2, 128)
 
     def lanes(c):
         return slice(c * 128, (c + 1) * 128)
 
-    def turn(c):
+    def turn(c, chosen):
         at = lanes(c)
         for l in DEGREES:
+            wanted = [a for a in orders(l) if a in chosen]
             sums = {}
             for b in range(-l, l + 1):
-                k = l * l + l + b
-                part = xs[k * 64 : (k + 1) * 64, at]
-                for a in orders(l):
+                if wanted:
+                    k = l * l + l + b
+                    part = xs[k * 64 : (k + 1) * 64, at]
+                for a in wanted:
                     e = entry(l, a, b)
                     term = dtab[e : e + 1, at] * part
                     sums[a] = sums[a] + term if a in sums else term
-            for a in orders(l):
+            for a in wanted:
                 rot[c, frame_slot(l, a), rep] = sums[a].astype(BF16)
 
-    def to_peer(c):
+    def to_peer(c, part):
+        rows = pl.ds(0, 7) if part == 0 else pl.ds(7, 22)
         return pltpu.make_async_remote_copy(
-            src_ref=rot.at[c, :, rep],
-            dst_ref=rot.at[c, :, rep],
-            send_sem=ps_sem.at[c],
-            recv_sem=pr_sem.at[c],
+            src_ref=rot.at[c, rows, rep],
+            dst_ref=rot.at[c, rows, rep],
+            send_sem=ps_sem.at[c, part],
+            recv_sem=pr_sem.at[c, part],
             device_id={"rep": 1 - rep},
             device_id_type=MESH,
         )
 
-    def send(r, plane, allowed, source, target, send_sem, recv_sem):
+    def swap_table(c):
+        return pltpu.make_async_remote_copy(
+            src_ref=dswap.at[c, rep],
+            dst_ref=dswap.at[c, rep],
+            send_sem=ws_sem.at[c],
+            recv_sem=wr_sem.at[c],
+            device_id={"rep": 1 - rep},
+            device_id_type=MESH,
+        )
+
+    def send(u, plane, allowed, ordered, source, target, send_sem, recv_sem):
+        r = u
+        if ordered:
+            row = ((u & 7) >> 1) ^ ((u & 7) >> 2)
+            ox = (u >> 3) * 2 + (u & 1)
+            ahead = ox * 4 + ((row - py - ox) & 3)
+            r = jnp.where(plane < 4, ahead, u)
         tx = (px + (r >> 2)) & 3
         ty = (py + r + (r >> 2)) & 3
         slot = r * 8 + ((plane - pz) & 7)
@@ -210,10 +236,10 @@
                 r = t
                 for early, gap in lead:
                     r = r + jnp.where(plane == early, t // gap, 0)
-                send(r, plane, r < 16, *buffers)
+                send(r, plane, r < 16, bool(lead), *buffers)
             for early, gap in lead:
                 r = t + t // gap + 1
-                send(r, early, (t % gap == gap - 1) & (r < 16), *buffers)
+                send(r, early, (t % gap == gap - 1) & (r < 16), True, *buffers)
             return carry
 
         lax.fori_loop(first, last, step, 0)
@@ -222,16 +248,21 @@
         part = buffer.at[pl.ds(c * CSLOTS, CSLOTS - 1 if c == 0 else CSLOTS)]
         pltpu.make_async_copy(part, part, sem.at[c]).wait()
 
+    def rows_of(c, first, count):
+        part = rot[c, first : first + count].reshape(count * 128, 128)
+        return nt(eye, part).astype(BF16)
+
+    def mix_zero():
+        for c in range(CHUNKS):
+            to_peer(c, 0).wait_recv()
+        zero = nt(jnp.concatenate([rows_of(c, 0, 7) for c in range(CHUNKS)], axis=0), wz[...])
+        message = jnp.concatenate([zero, jnp.zeros((ROWS, 64), F32)], axis=1)
+        zsend[...] = message.astype(BF16).reshape(SLOTS, 2, ZERO_TILES * 128)
+
     def mix(c):
-        to_peer(c).wait_recv()
-
-        def rows(first, count):
-            part = rot[c, first : first + count].reshape(count * 128, 128)
-            return nt(eye, part).astype(BF16)
-
-        zero = nt(rows(0, 7), wz[...])
-        one = jnp.concatenate([rows(7, 6), rows(13, 6)], axis=0)
-        two = jnp.concatenate([rows(19, 5), rows(24, 5)], axis=0)
+        to_peer(c, 1).wait_recv()
+        one = jnp.concatenate([rows_of(c, 7, 6), rows_of(c, 13, 6)], axis=0)
+        two = jnp.concatenate([rows_of(c, 19, 5), rows_of(c, 24, 5)], axis=0)
         first, second = nn(one, w1[0]), nn(one, w1[1])
         plus1 = first[0:128] - second[128:256]
         minus1 = second[0:128] + first[128:256]
@@ -239,30 +270,43 @@
         plus2 = first[0:128] - second[128:256]
         minus2 = second[0:128] + first[128:256]
         last = jnp.concatenate([plus2[:, 256:320], minus2[:, 256:320]], axis=1)
-        tail = jnp.concatenate([zero[:, 384:448], jnp.zeros((CROWS, 64), F32)], axis=1)
-        pieces = [zero[:, 0:384], plus1, minus1, plus2[:, 0:256], minus2[:, 0:256], last, tail]
         spot = 0
-        for piece in pieces:
+        for piece in (plus1, minus1, plus2[:, 0:256], minus2[:, 0:256], last):
             wide = piece.shape[1]
             msend[c * CSLOTS : (c + 1) * CSLOTS, :, spot : spot + wide] = piece.astype(BF16).reshape(
                 CSLOTS, 2, wide
             )
             spot += wide
 
-    def unturn(c):
-        at = lanes(c)
+    def table_in(c):
         wait_chunk(c, drecv, dr_sem)
         if c == 0:
             drecv[0] = dsend[0]
-        rows = drecv[c * CSLOTS : (c + 1) * CSLOTS].reshape(CROWS, 256)
-        dtab[0:128, at] = nt(eye, rows[:, 0:128])
-        dtab[128:256, at] = nt(eye, rows[:, 128:256])
+        rows = drecv[c * CSLOTS : (c + 1) * CSLOTS].reshape(CROWS, 128)
+        dswap[c, rep] = nt(eye, rows).astype(BF16)
+        swap_table(c).start()
+
+    def tiles_in(c, buffer, count, first):
+        for t in range(count):
+            tile = buffer[c * CSLOTS : (c + 1) * CSLOTS, :, t * 128 : (t + 1) * 128].reshape(CROWS, 128)
+            xs[(first + t) * 128 : (first + t + 1) * 128, lanes(c)] = nt(eye, tile)
+
+    def zero_in(c):
+        at = lanes(c)
+        swap_table(c).wait_recv()
+        dtab[0:128, at] = dswap[c, 0].astype(F32)
+        dtab[128:256, at] = dswap[c, 1].astype(F32)
+        wait_chunk(c, zrecv, zr_sem)
+        if c == 0:
+            zrecv[0] = zsend[0]
+        tiles_in(c, zrecv, ZERO_TILES, 0)
+
+    def unturn(c):
+        at = lanes(c)
         wait_chunk(c, mrecv, mr_sem)
         if c == 0:
             mrecv[0] = msend[0]
-        for t in range(TILES):
-            tile = mrecv[c * CSLOTS : (c + 1) * CSLOTS, :, t * 128 : (t + 1) * 128].reshape(CROWS, 128)
-            xs[t * 128 : (t + 1) * 128, at] = nt(eye, tile)
+        tiles_in(c, mrecv, REST_TILES, ZERO_TILES)
         for l in DEGREES:
             parts = {}
             for a in orders(l):
@@ -278,16 +322,22 @@
                 k = l * l + l + b
                 back[k * 64 : (k + 1) * 64, at] = total.astype(BF16)
 
-    for c in range(CHUNKS):
-        turn(c)
+    others = (-2, -1, 1, 2)
+    for c in range(CHUNKS):
+        turn(c, (0,))
 
     pl.semaphore_wait(barrier, SLOTS)
     for c in range(CHUNKS):
-        to_peer(c).start()
+        to_peer(c, 0).start()
     send_steps(0, 16, (dsend, drecv, ds_sem, dr_sem), ())
+    for c in range(CHUNKS):
+        turn(c, others)
+        to_peer(c, 1).start()
 
     for copy in loads[5:]:
         copy.wait()
+    mix_zero()
+    send_steps(0, 16, (zsend, zrecv, zs_sem, zr_sem), LEAD)
     mix(0)
     send_steps(0, 4, (msend, mrecv, ms_sem, mr_sem), LEAD)
     mix(1)
@@ -299,6 +349,10 @@
     )
     hot_n = nt(hot_d, perm_back).astype(BF16)
 
+    for c in range(CHUNKS):
+        table_in(c)
+    for c in range(CHUNKS):
+        zero_in(c)
     square = jnp.zeros((64, 1), F32)
     for c in range(CHUNKS):
         unturn(c)
@@ -321,8 +375,11 @@
     )
     swap.start()
     for c in range(CHUNKS):
-        to_peer(c).wait_send()
+        to_peer(c, 0).wait_send()
+        to_peer(c, 1).wait_send()
+        swap_table(c).wait_send()
         wait_chunk(c, dsend, ds_sem)
+        wait_chunk(c, zsend, zs_sem)
         wait_chunk(c, msend, ms_sem)
     swap.wait()
     mean = (sqs[...] + sqr[...]) / 6272.0
@@ -363,15 +420,22 @@
             pltpu.VMEM((256, ROWS), F32),
             pltpu.VMEM((WIDTH, ROWS), F32),
             pltpu.VMEM((CHUNKS, 29, 2, 64, 128), BF16),
-            pltpu.VMEM((SLOTS, 2, TILES * 128), BF16),
-            pltpu.VMEM((SLOTS, 2, TILES * 128), BF16),
-            pltpu.VMEM((SLOTS, 2, 256), BF16),
-            pltpu.VMEM((SLOTS, 2, 256), BF16),
+            pltpu.VMEM((SLOTS, 2, ZERO_TILES * 128), BF16),
+            pltpu.VMEM((SLOTS, 2, ZERO_TILES * 128), BF16),
+            pltpu.VMEM((SLOTS, 2, REST_TILES * 128), BF16),
+            pltpu.VMEM((SLOTS, 2, REST_TILES * 128), BF16),
+            pltpu.VMEM((SLOTS, 2, 128), BF16),
+            pltpu.VMEM((SLOTS, 2, 128), BF16),
+            pltpu.VMEM((CHUNKS, 2, 128, 128), BF16),
             pltpu.VMEM((WIDTH, ROWS), BF16),
             pltpu.VMEM((64, WIDTH), F32),
             pltpu.VMEM((64, 128), F32),
             pltpu.VMEM((64, 128), F32),
             dma((9,)),
+            dma((CHUNKS, 2)),
+            dma((CHUNKS, 2)),
+            dma((CHUNKS,)),
+            dma((CHUNKS,)),
             dma((CHUNKS,)),
             dma((CHUNKS,)),
             dma((CHUNKS,)),

time: 43.7 us -> 42.4 us (0.970)
  the two profiles are of different devices: /device:TPU:35 before, /device:TPU:49 now
where the time goes in v4:
time: 42.4 us; the launch traced here: 42.3 us
  Pallas kernels  41.6 us (98%)
  local copies, waits for them, and re-layouts  0.75 us (2%)
    pallas_call x1, Pallas kernels, shards(): pl.pallas_call(kernel, out_shape=jax.ShapeDtypeStruct((64, WIDTH), BF16),...  41.6 us

profile of v4, /device:TPU:49, one launch (start us, length us, event | category | flops | bytes accessed | tf_op | source)
XLA Modules:
  0.0 42.3 jit_solution(4258734322933359463)
XLA Ops:
  0.0 41.6 %shard_map.91 = bf16[64,3136]{1,0:T(8,128)(2,1)S(1)} custom-call(bf16[64,3136]{1,0:T(8,128)(2,1)} %bitcast.24, bf16[235,2,128]{2,1,0:T(2,128)(2,1)} %bitcast.25, s32[2,128]{1,0:T(2,128)} %bitcast.26, s32[2,128]{1,0:T(2,128)} %bitcast.27, s32[1,128]{1,0:T(1,128)} %cnt_hbm.1, bf16[448,896]{1,0:T(8,128)(2,1)} %bitcast.23, bf16[2,768,384]{2,1,0:T(8,128)(2,1)} %bitcast.21, ...), custom_call_target="tpu_custom_call" | custom-call | tf_op jit(solution)/shard_map/pallas_call | solution.py:404
  41.6 0.8 %copy.12 = bf16[64,1,3136]{2,0,1:T(8,128)(2,1)} copy(bf16[64,1,3136]{2,0,1:T(8,128)(2,1)S(1)} %bitcast.20) | data formatting | bytes 802816

commit v5 on v4

--- a/solution.py
+++ b/solution.py
@@ -85,8 +85,8 @@
     x_hbm, rt_hbm, src_hbm, dst_hbm, cnt_hbm, wz_hbm, w1_hbm, w2_hbm, gain_hbm,
     out_ref,
     xv, rtv, srcv, dstv, cntv, wz, w1, w2, gain,
-    rts, dtab, xs, rot, zsend, zrecv, msend, mrecv, dsend, drecv, dswap, back, agg, sqs, sqr,
-    load_sem, ps_sem, pr_sem, zs_sem, zr_sem, ms_sem, mr_sem, ds_sem, dr_sem, ws_sem, wr_sem, q_sem,
+    rts, dtab, xs, rot, zsend, zrecv, msend, mrecv, dsend, drecv, dswap, sswap, back, agg, sqs, sqr,
+    load_sem, ps_sem, pr_sem, zs_sem, zr_sem, ms_sem, mr_sem, ds_sem, dr_sem, ws_sem, wr_sem, vs_sem, vr_sem, q_sem,
 ):
     me = lax.axis_index("dev")
     rep = lax.axis_index("rep")
@@ -162,8 +162,9 @@
         rts[0:235, i * 128 : (i + 1) * 128] = rtv[:, i, :].astype(F32)
     table = rts[...].astype(BF16)
     dtab[...] = nt(table, perm)
-    half = rts[pl.ds(pl.multiple_of(rep * 128, 128), 128), :].astype(BF16)
-    dsend[...] = nt(perm, half).astype(BF16).reshape(SLOTS, 2, 128)
+    share = rts[pl.ds(pl.multiple_of(rep * 64, 64), 64), :].astype(BF16)
+    spare = nt(perm, share)
+    dsend[...] = nt(perm, table[128:256]).astype(BF16).reshape(SLOTS, 2, 128)
 
     def lanes(c):
         return slice(c * 128, (c + 1) * 128)
@@ -197,10 +198,20 @@
 
     def swap_table(c):
         return pltpu.make_async_remote_copy(
-            src_ref=dswap.at[c, rep],
-            dst_ref=dswap.at[c, rep],
+            src_ref=dswap.at[c],
+            dst_ref=dswap.at[c],
             send_sem=ws_sem.at[c],
             recv_sem=wr_sem.at[c],
+            device_id={"rep": 1 - rep},
+            device_id_type=MESH,
+        )
+
+    def swap_spare(c):
+        return pltpu.make_async_remote_copy(
+            src_ref=sswap.at[c, rep],
+            dst_ref=sswap.at[c, rep],
+            send_sem=vs_sem.at[c],
+            recv_sem=vr_sem.at[c],
             device_id={"rep": 1 - rep},
             device_id_type=MESH,
         )
@@ -256,7 +267,7 @@
         for c in range(CHUNKS):
             to_peer(c, 0).wait_recv()
         zero = nt(jnp.concatenate([rows_of(c, 0, 7) for c in range(CHUNKS)], axis=0), wz[...])
-        message = jnp.concatenate([zero, jnp.zeros((ROWS, 64), F32)], axis=1)
+        message = jnp.concatenate([zero, spare], axis=1)
         zsend[...] = message.astype(BF16).reshape(SLOTS, 2, ZERO_TILES * 128)
 
     def mix(c):
@@ -279,12 +290,14 @@
             spot += wide
 
     def table_in(c):
-        wait_chunk(c, drecv, dr_sem)
-        if c == 0:
-            drecv[0] = dsend[0]
-        rows = drecv[c * CSLOTS : (c + 1) * CSLOTS].reshape(CROWS, 128)
-        dswap[c, rep] = nt(eye, rows).astype(BF16)
-        swap_table(c).start()
+        @pl.when(rep == 0)
+        def _():
+            wait_chunk(c, drecv, dr_sem)
+            if c == 0:
+                drecv[0] = dsend[0]
+            rows = drecv[c * CSLOTS : (c + 1) * CSLOTS].reshape(CROWS, 128)
+            dswap[c] = nt(eye, rows).astype(BF16)
+            swap_table(c).start()
 
     def tiles_in(c, buffer, count, first):
         for t in range(count):
@@ -292,14 +305,24 @@
             xs[(first + t) * 128 : (first + t + 1) * 128, lanes(c)] = nt(eye, tile)
 
     def zero_in(c):
-        at = lanes(c)
-        swap_table(c).wait_recv()
-        dtab[0:128, at] = dswap[c, 0].astype(F32)
-        dtab[128:256, at] = dswap[c, 1].astype(F32)
         wait_chunk(c, zrecv, zr_sem)
         if c == 0:
             zrecv[0] = zsend[0]
         tiles_in(c, zrecv, ZERO_TILES, 0)
+        sswap[c, rep] = xs[448:512, lanes(c)].astype(BF16)
+        swap_spare(c).start()
+
+    def table_done(c):
+        at = lanes(c)
+
+        @pl.when(rep == 1)
+        def _():
+            swap_table(c).wait_recv()
+
+        swap_spare(c).wait_recv()
+        dtab[0:64, at] = sswap[c, 0].astype(F32)
+        dtab[64:128, at] = sswap[c, 1].astype(F32)
+        dtab[128:256, at] = dswap[c].astype(F32)
 
     def unturn(c):
         at = lanes(c)
@@ -329,7 +352,11 @@
     pl.semaphore_wait(barrier, SLOTS)
     for c in range(CHUNKS):
         to_peer(c, 0).start()
-    send_steps(0, 16, (dsend, drecv, ds_sem, dr_sem), ())
+
+    @pl.when(rep == 0)
+    def _():
+        send_steps(0, 16, (dsend, drecv, ds_sem, dr_sem), ())
+
     for c in range(CHUNKS):
         turn(c, others)
         to_peer(c, 1).start()
@@ -353,6 +380,8 @@
         table_in(c)
     for c in range(CHUNKS):
         zero_in(c)
+    for c in range(CHUNKS):
+        table_done(c)
     square = jnp.zeros((64, 1), F32)
     for c in range(CHUNKS):
         unturn(c)
@@ -377,8 +406,13 @@
     for c in range(CHUNKS):
         to_peer(c, 0).wait_send()
         to_peer(c, 1).wait_send()
-        swap_table(c).wait_send()
-        wait_chunk(c, dsend, ds_sem)
+        swap_spare(c).wait_send()
+
+        @pl.when(rep == 0)
+        def _():
+            swap_table(c).wait_send()
+            wait_chunk(c, dsend, ds_sem)
+
         wait_chunk(c, zsend, zs_sem)
         wait_chunk(c, msend, ms_sem)
     swap.wait()
@@ -426,7 +460,8 @@
             pltpu.VMEM((SLOTS, 2, REST_TILES * 128), BF16),
             pltpu.VMEM((SLOTS, 2, 128), BF16),
             pltpu.VMEM((SLOTS, 2, 128), BF16),
-            pltpu.VMEM((CHUNKS, 2, 128, 128), BF16),
+            pltpu.VMEM((CHUNKS, 128, 128), BF16),
+            pltpu.VMEM((CHUNKS, 2, 64, 128), BF16),
             pltpu.VMEM((WIDTH, ROWS), BF16),
             pltpu.VMEM((64, WIDTH), F32),
             pltpu.VMEM((64, 128), F32),
@@ -434,6 +469,8 @@
             dma((9,)),
             dma((CHUNKS, 2)),
             dma((CHUNKS, 2)),
+            dma((CHUNKS,)),
+            dma((CHUNKS,)),
             dma((CHUNKS,)),
             dma((CHUNKS,)),
             dma((CHUNKS,)),

time: 42.4 us -> 42 us (level)
  no operation moved by 1% of the time
where the time goes in v5:
time: 42 us; the launch traced here: 41.9 us
  Pallas kernels  41.2 us (98%)
  local copies, waits for them, and re-layouts  0.75 us (2%)
    pallas_call x1, Pallas kernels, shards(): pl.pallas_call(kernel, out_shape=jax.ShapeDtypeStruct((64, WIDTH), BF16),...  41.2 us

profile of v5, /device:TPU:49, one launch (start us, length us, event | category | flops | bytes accessed | tf_op | source)
XLA Modules:
  0.0 41.9 jit_solution(3602447349993984430)
XLA Ops:
  0.0 41.2 %shard_map.91 = bf16[64,3136]{1,0:T(8,128)(2,1)S(1)} custom-call(bf16[64,3136]{1,0:T(8,128)(2,1)} %bitcast.24, bf16[235,2,128]{2,1,0:T(2,128)(2,1)} %bitcast.25, s32[2,128]{1,0:T(2,128)} %bitcast.26, s32[2,128]{1,0:T(2,128)} %bitcast.27, s32[1,128]{1,0:T(1,128)} %cnt_hbm.1, bf16[448,896]{1,0:T(8,128)(2,1)} %bitcast.23, bf16[2,768,384]{2,1,0:T(8,128)(2,1)} %bitcast.21, ...), custom_call_target="tpu_custom_call" | custom-call | tf_op jit(solution)/shard_map/pallas_call | solution.py:438
  41.2 0.8 %copy.12 = bf16[64,1,3136]{2,0,1:T(8,128)(2,1)} copy(bf16[64,1,3136]{2,0,1:T(8,128)(2,1)S(1)} %bitcast.20) | data formatting | bytes 802816

commit v6 on v5

--- a/solution.py
+++ b/solution.py
@@ -107,7 +107,8 @@
 
         return carry
 
-    lax.fori_loop(0, 16, greet, 0)
+    for g in range(16):
+        greet(g, 0)
     pl.semaphore_signal(barrier, inc=1, device_id={"rep": 1 - rep}, device_id_type=MESH)
 
     loads = [

time: 42 us -> 41.8 us (level)
  no operation moved by 1% of the time
where the time goes in v6:
time: 41.8 us; the launch traced here: 41.7 us
  Pallas kernels  40.9 us (98%)
  local copies, waits for them, and re-layouts  0.75 us (2%)
    pallas_call x1, Pallas kernels, shards(): pl.pallas_call(kernel, out_shape=jax.ShapeDtypeStruct((64, WIDTH), BF16),...  40.9 us

profile of v6, /device:TPU:49, one launch (start us, length us, event | category | flops | bytes accessed | tf_op | source)
XLA Modules:
  0.0 41.7 jit_solution(8620566597360030082)
XLA Ops:
  0.0 40.9 %shard_map.91 = bf16[64,3136]{1,0:T(8,128)(2,1)S(1)} custom-call(bf16[64,3136]{1,0:T(8,128)(2,1)} %bitcast.24, bf16[235,2,128]{2,1,0:T(2,128)(2,1)} %bitcast.25, s32[2,128]{1,0:T(2,128)} %bitcast.26, s32[2,128]{1,0:T(2,128)} %bitcast.27, s32[1,128]{1,0:T(1,128)} %cnt_hbm.1, bf16[448,896]{1,0:T(8,128)(2,1)} %bitcast.23, bf16[2,768,384]{2,1,0:T(8,128)(2,1)} %bitcast.21, ...), custom_call_target="tpu_custom_call" | custom-call | tf_op jit(solution)/shard_map/pallas_call | solution.py:439
  41.0 0.8 %copy.12 = bf16[64,1,3136]{2,0,1:T(8,128)(2,1)} copy(bf16[64,1,3136]{2,0,1:T(8,128)(2,1)S(1)} %bitcast.20) | data formatting | bytes 802816
